TPU v7x, 32 devices: a whole 2x2x4 slice. The times are simulated.
32 devices in a mesh: rep: 4 (over y, x), shard: 4 (over z), tp: 2 (over core).
Axes of the slice: x: 2, y: 2, z: 4, core: 2. Of those that a mesh axis runs over, the one named last changes fastest.
Arguments:
- x_in: bfloat16 [4, 1536, 1536], P('rep', 'shard'), may hold values from -6 to 6
- query_key_value_weight: bfloat16 [2, 1536, 2048], P(None, 'shard', 'tp'), may hold values from -0.15625 to 0.15625
- qkv_bias: bfloat16 [2, 2048], P(None, 'tp'), may hold values from -3 to 3
- output_weight: bfloat16 [2, 1536, 1536], P(None, 'shard', 'tp'), may hold values from -0.875 to 0.875
- feedforward_entry_matrix: bfloat16 [2, 1536, 2, 8960], P(None, 'shard', None, 'tp'), may hold values from -0.15625 to 0.15625
- down_weight: bfloat16 [2, 1536, 8960], P(None, 'shard', 'tp'), may hold values from -0.125 to 0.125
- norm_gains: bfloat16 [2, 2, 1536], replicated, may hold values from 0.5 to 1.5
- piece_starts: int32 [4, 2], P('rep'), may hold values from 0 to 1280, as said below
- seq_lengths: int32 [4], P('rep'), may hold values from 1 to 1536, 4608 in all
- grad_out: bfloat16 [4, 1536, 1536], P('rep', 'shard'), may hold values from -6 to 6
Outputs:
- out_act: bfloat16 [4, 1536, 1536], P('rep', 'shard')
- grad_input: float32 [4, 1536, 1536], P('rep', 'shard')
- grad_qkv: float32 [2, 1536, 2048], P(None, 'shard', 'tp')
- grad_bias: float32 [2, 2048], P(None, 'tp')
- grad_out_proj: float32 [2, 1536, 1536], P(None, 'shard', 'tp')
- grad_gate_up: float32 [2, 1536, 2, 8960], P(None, 'shard', None, 'tp')
- grad_down: float32 [2, 1536, 8960], P(None, 'shard', 'tp')
- grad_gains: float32 [2, 2, 1536], replicated
Inputs may be any that keep to these rules, and one draw needn't show every extreme that they name: `piece_starts`: piece k of a sequence starts between k * 768 and (k + 1) * 768 - 256, so pieces never intersect.
All inputs are finite; a program needn't handle non-finite values. No bound on the sum of `seq_lengths` on one device may be relied on, other than what follows from the above.
Results may differ from a plain program's by a relative error of at most 0.017.
Values may be sent and summed in bfloat16 or wider, within the bound.
A program may use at most 512 MiB of HBM per device.

v0:
```python
import functools
import math

import jax
import jax.numpy as jnp
from jax import lax
from jax.experimental import pallas as pl
from jax.experimental.pallas import tpu as pltpu
from jax.sharding import PartitionSpec as P


QUERY_HEADS = 12
KEY_VALUE_HEADS = 2
HEAD_SIZE = 128
LAYERS = 2
PIECE = 256
PIECES = 2
LANES = 128


EPS = 1e-06
THETA = 1000000.0


def rope_tables(positions):
    freq = jnp.exp(
        jnp.arange(HEAD_SIZE // 2, dtype=jnp.float32) * (-2.0 * math.log(THETA) / HEAD_SIZE)
    )
    angle = positions.astype(jnp.float32)[:, None] * freq[None, :]
    angle = jnp.concatenate([angle, angle], axis=1)
    return (jnp.cos(angle), jnp.sin(angle))


def rotate(content_entries, cosine, sine):
    half = content_entries.shape[-1] // 2
    turned = jnp.concatenate([-content_entries[..., half:], content_entries[..., :half]], axis=-1)
    return content_entries * cosine + turned * sine


def rotate_back(grads, cosine, sine):
    half = grads.shape[-1] // 2
    shifted = grads * sine
    return grads * cosine + jnp.concatenate([shifted[..., half:], -shifted[..., :half]], axis=-1)


def piece_ids(positions, starts):
    inside = (positions[..., :, None] >= starts[..., None, :]) & (
        positions[..., :, None] < starts[..., None, :] + PIECE
    )
    labels = jnp.arange(1, PIECES + 1, dtype=jnp.int32)
    return jnp.sum(jnp.where(inside, labels, 0), axis=-1)


def norm_scale(content_entries):
    return lax.rsqrt(jnp.mean(content_entries * content_entries, axis=-1, keepdims=True) + EPS)


def norm_back(content_entries, scale, gain, grad_normed):
    inner = jnp.mean(grad_normed * gain * content_entries, axis=-1, keepdims=True)
    grad_values = scale * gain * grad_normed - content_entries * (scale * scale * scale) * inner
    gain_grad = jnp.sum(grad_normed * content_entries * scale, axis=0)
    return (grad_values, gain_grad)


def masked_scores(query_rows, keys_all, seen, root):
    raw = (
        jnp.einsum("sqgjd,skgd->sgjqk", query_rows, keys_all, preferred_element_type=jnp.float32)
        / root
    )
    return jnp.where(seen[:, None, None], raw, -1e30)


MESH = pl.DeviceIdType.MESH
FAST_BYTES_PER_US = 3_000_000


def left_product(left, right):
    return lax.dot_general(
        left, right, (((0,), (0,)), ((), ())), preferred_element_type=jnp.float32
    ).astype(jnp.bfloat16)


def right_product(left, right):
    return lax.dot_general(
        left, right, (((1,), (1,)), ((), ())), preferred_element_type=jnp.float32
    )


def product(left, right):
    return jnp.dot(left, right, preferred_element_type=jnp.float32)


def next_on(axis, step):
    return {axis: lax.rem(lax.axis_index(axis) + step, lax.axis_size(axis))}


def greet(sizes):
    barrier = pltpu.get_barrier_semaphore()
    for axis, count in sizes:
        for step in range(1, count):
            pl.semaphore_signal(
                barrier, inc=1, device_id=next_on(axis, step), device_id_type=MESH
            )
    pl.semaphore_wait(barrier, sum(count - 1 for _, count in sizes))


def start_copy(source, target, sent, received, device):
    copy = pltpu.make_async_remote_copy(
        src_ref=source,
        dst_ref=target,
        send_sem=sent,
        recv_sem=received,
        device_id=device,
        device_id_type=MESH,
    )
    copy.start()
    return copy


def by_rows(rows, update):
    size = next((size for size in (32, 16) if rows % size == 0), rows)

    def step(index, carry):
        update(pl.ds(pl.multiple_of(index * size, size), size))
        return carry

    lax.fori_loop(0, rows // size, step, 0)


def call_kernel(kernel, name, out_shape, scratch, operands, micros):
    return pl.pallas_call(
        kernel,
        out_shape=out_shape,
        in_specs=[pl.BlockSpec(memory_space=pltpu.VMEM)] * len(operands),
        out_specs=pl.BlockSpec(memory_space=pltpu.VMEM),
        scratch_shapes=scratch,
        compiler_params=pltpu.CompilerParams(
            collective_id=name, has_side_effects=True, vmem_limit_bytes=40 * 1024 * 1024
        ),
        cost_estimate=pl.CostEstimate(
            flops=0, bytes_accessed=int(micros * FAST_BYTES_PER_US), transcendentals=0
        ),
    )(*operands)


def ring_gather_kernel(axis, count, x_ref, out_ref, sent, received):
    greet(((axis, count),))
    copies = [
        start_copy(
            x_ref,
            out_ref.at[count - step],
            sent.at[step],
            received.at[count - step],
            next_on(axis, step),
        )
        for step in range(1, count)
    ]
    out_ref[0] = x_ref[...]
    for copy in copies:
        copy.wait()


def ring_gather(values, axis, name, micros):
    count = lax.axis_size(axis)
    if count == 1:
        return values[None]
    return call_kernel(
        functools.partial(ring_gather_kernel, axis, count),
        name,
        jax.ShapeDtypeStruct((count, *values.shape), values.dtype),
        [pltpu.SemaphoreType.DMA((count,)), pltpu.SemaphoreType.DMA((count,))],
        (values,),
        micros,
    )


def ring_scatter_kernel(axis, count, far_ref, near_ref, out_ref, arrived, sent, received):
    greet(((axis, count),))
    copies = [
        start_copy(
            far_ref.at[step - 1],
            arrived.at[step - 1],
            sent.at[step],
            received.at[step],
            next_on(axis, step),
        )
        for step in range(1, count)
    ]
    for copy in copies:
        copy.wait()

    def add(some):
        total = near_ref[some, :]
        for step in range(1, count):
            total = total + arrived[step - 1, some, :].astype(jnp.float32)
        out_ref[some, :] = total

    by_rows(near_ref.shape[0], add)


def ring_scatter(far, near, axis, name, micros):
    count = lax.axis_size(axis)
    if count == 1:
        return near
    return call_kernel(
        functools.partial(ring_scatter_kernel, axis, count),
        name,
        jax.ShapeDtypeStruct(near.shape, jnp.float32),
        [
            pltpu.VMEM(far.shape, far.dtype),
            pltpu.SemaphoreType.DMA((count,)),
            pltpu.SemaphoreType.DMA((count,)),
        ],
        (far, near),
        micros,
    )


def plane_gather_kernel(reps, cores, x_ref, out_ref, sent, received, sent_on, received_on):
    greet((("rep", reps), ("tp", cores)))
    copies = [
        start_copy(
            x_ref,
            out_ref.at[0, reps - step],
            sent.at[step],
            received.at[reps - step],
            next_on("rep", step),
        )
        for step in range(1, reps)
    ]
    passed = []

    def pass_on(source, slot):
        for step in range(1, cores):
            passed.append(
                start_copy(
                    source,
                    out_ref.at[cores - step, slot],
                    sent_on.at[step, slot],
                    received_on.at[cores - step, slot],
                    next_on("tp", step),
                )
            )

    pass_on(x_ref, 0)
    out_ref[0, 0] = x_ref[...]
    for copy, step in zip(copies, range(1, reps)):
        copy.wait_recv()
        pass_on(out_ref.at[0, reps - step], reps - step)
    for copy in copies:
        copy.wait_send()
    for copy in passed:
        copy.wait()


def plane_gather(rows):
    reps, cores = lax.axis_size("rep"), lax.axis_size("tp")
    gathered = call_kernel(
        functools.partial(plane_gather_kernel, reps, cores),
        1,
        jax.ShapeDtypeStruct((cores, reps, *rows.shape), rows.dtype),
        [
            pltpu.SemaphoreType.DMA((reps,)),
            pltpu.SemaphoreType.DMA((reps,)),
            pltpu.SemaphoreType.DMA((cores, reps)),
            pltpu.SemaphoreType.DMA((cores, reps)),
        ],
        (rows,),
        30,
    )
    return gathered.reshape(cores * reps * rows.shape[0], rows.shape[1])


def plane_scatter_kernel(
    reps,
    cores,
    far_ref,
    near_ref,
    out_ref,
    arrived,
    staged,
    landed,
    sent,
    received,
    sent_on,
    received_on,
):
    greet((("rep", reps), ("tp", cores)))
    rows = near_ref.shape[1]
    order = list(range(1, reps)) + [0]
    first = {}
    for slot in order:
        for step in range(1, cores):
            first[step, slot] = start_copy(
                far_ref.at[step - 1, slot],
                arrived.at[step - 1, slot],
                sent.at[step, slot],
                received.at[step, slot],
                next_on("tp", step),
            )

    def near_sum(slot, some):
        total = near_ref[slot, some, :]
        for step in range(1, cores):
            total = total + arrived[step - 1, slot, some, :].astype(jnp.float32)
        return total

    second = []
    for slot in order:
        for step in range(1, cores):
            first[step, slot].wait_recv()
        if slot:

            def stage(some, slot=slot):
                staged[slot - 1, some, :] = near_sum(slot, some).astype(jnp.bfloat16)

            by_rows(rows, stage)
            second.append(
                start_copy(
                    staged.at[slot - 1],
                    landed.at[slot - 1],
                    sent_on.at[slot],
                    received_on.at[slot],
                    next_on("rep", slot),
                )
            )
    for copy in first.values():
        copy.wait_send()
    for copy in second:
        copy.wait()

    def finish(some):
        total = near_sum(0, some)
        for slot in range(1, reps):
            total = total + landed[slot - 1, some, :].astype(jnp.float32)
        out_ref[some, :] = total

    by_rows(rows, finish)


def plane_scatter(far, near):
    reps, cores = lax.axis_size("rep"), lax.axis_size("tp")
    rows = near.shape[0] // reps
    far = far.reshape(cores - 1, reps, rows, far.shape[1])
    near = near.reshape(reps, rows, near.shape[1])
    return call_kernel(
        functools.partial(plane_scatter_kernel, reps, cores),
        2,
        jax.ShapeDtypeStruct(near.shape[1:], jnp.float32),
        [
            pltpu.VMEM(far.shape, jnp.bfloat16),
            pltpu.VMEM((reps - 1, *near.shape[1:]), jnp.bfloat16),
            pltpu.VMEM((reps - 1, *near.shape[1:]), jnp.bfloat16),
            pltpu.SemaphoreType.DMA((cores, reps)),
            pltpu.SemaphoreType.DMA((cores, reps)),
            pltpu.SemaphoreType.DMA((reps,)),
            pltpu.SemaphoreType.DMA((reps,)),
        ],
        (far, near),
        35,
    )


def weight_gather_kernel(
    shards, reps, w_ref, out_ref, sent, received, sent_on, received_on
):
    greet((("shard", shards), ("rep", reps)))
    place = lax.axis_index("shard")
    replica = lax.axis_index("rep")
    copies = [
        start_copy(
            w_ref.at[replica],
            out_ref.at[place, replica],
            sent.at[step],
            received.at[step],
            next_on("shard", step),
        )
        for step in range(1, shards)
    ]
    out_ref[place] = w_ref[...]
    passed = []
    for step in range(1, shards):
        copies[step - 1].wait_recv()
        source = out_ref.at[lax.rem(place + shards - step, shards), replica]
        for far in range(1, reps):
            passed.append(
                start_copy(
                    source,
                    source,
                    sent_on.at[step, far],
                    received_on.at[step, far],
                    next_on("rep", far),
                )
            )
    for copy in copies:
        copy.wait_send()
    for copy in passed:
        copy.wait()


def weight_gather(weight):
    shards, reps = lax.axis_size("shard"), lax.axis_size("rep")
    depth, columns = weight.shape
    parts = weight.reshape(reps, depth // reps, columns)
    gathered = call_kernel(
        functools.partial(weight_gather_kernel, shards, reps),
        9,
        jax.ShapeDtypeStruct((shards, *parts.shape), weight.dtype),
        [
            pltpu.SemaphoreType.DMA((shards,)),
            pltpu.SemaphoreType.DMA((shards,)),
            pltpu.SemaphoreType.DMA((shards, reps)),
            pltpu.SemaphoreType.DMA((shards, reps)),
        ],
        (parts,),
        50,
    )
    return gathered.reshape(shards * depth, columns)


def gradient_sum_kernel(
    shards,
    reps,
    grad_ref,
    out_ref,
    arrived,
    staged,
    landed,
    summed,
    sent,
    received,
    sent_far,
    received_far,
    sent_on,
    received_on,
):
    greet((("shard", shards), ("rep", reps)))
    place = lax.axis_index("shard")
    replica = lax.axis_index("rep")
    rows = grad_ref.shape[2]
    order = list(range(1, shards)) + [0]
    first = {}
    for step in order:
        target = lax.rem(place + step, shards)
        for far in range(1, reps):
            first[step, far] = start_copy(
                grad_ref.at[target, lax.rem(replica + far, reps)],
                arrived.at[far - 1, step],
                sent.at[step, far],
                received.at[step, far],
                next_on("rep", far),
            )

    def replica_sum(step, some):
        target = lax.rem(place + step, shards)
        total = grad_ref[target, replica, some, :].astype(jnp.float32)
        for far in range(1, reps):
            total = total + arrived[far - 1, step, some, :].astype(jnp.float32)
        return total

    second = []
    for step in order:
        for far in range(1, reps):
            first[step, far].wait_recv()
        if step:

            def stage(some, step=step):
                staged[step - 1, some, :] = replica_sum(step, some).astype(jnp.bfloat16)

            by_rows(rows, stage)
            second.append(
                start_copy(
                    staged.at[step - 1],
                    landed.at[step - 1],
                    sent_far.at[step],
                    received_far.at[step],
                    next_on("shard", step),
                )
            )
    for copy in second:
        copy.wait()

    def finish(some):
        total = replica_sum(0, some)
        for step in range(1, shards):
            total = total + landed[step - 1, some, :].astype(jnp.float32)
        summed[some, :] = total.astype(jnp.bfloat16)

    by_rows(rows, finish)
    third = [
        start_copy(
            summed,
            out_ref.at[replica],
            sent_on.at[far],
            received_on.at[far],
            next_on("rep", far),
        )
        for far in range(1, reps)
    ]
    out_ref[replica] = summed[...]
    for copy in first.values():
        copy.wait_send()
    for copy in third:
        copy.wait()


def gradient_sum(grad):
    shards, reps = lax.axis_size("shard"), lax.axis_size("rep")
    columns = grad.shape[1]
    depth = grad.shape[0] // shards
    piece = (depth // reps, columns)
    summed = call_kernel(
        functools.partial(gradient_sum_kernel, shards, reps),
        10,
        jax.ShapeDtypeStruct((reps, *piece), grad.dtype),
        [
            pltpu.VMEM((reps - 1, shards, *piece), grad.dtype),
            pltpu.VMEM((shards - 1, *piece), grad.dtype),
            pltpu.VMEM((shards - 1, *piece), grad.dtype),
            pltpu.VMEM(piece, grad.dtype),
            pltpu.SemaphoreType.DMA((shards, reps)),
            pltpu.SemaphoreType.DMA((shards, reps)),
            pltpu.SemaphoreType.DMA((shards,)),
            pltpu.SemaphoreType.DMA((shards,)),
            pltpu.SemaphoreType.DMA((reps,)),
            pltpu.SemaphoreType.DMA((reps,)),
        ],
        (grad.reshape(shards, reps, *piece),),
        90,
    )
    return summed.reshape(depth, columns)


def sum_kernel(sizes, x_ref, out_ref, *scratch):
    greet(sizes)
    held = x_ref
    for place, (axis, count) in enumerate(sizes):
        total_ref, arrived, sent, received = scratch[4 * place : 4 * place + 4]
        copies = [
            start_copy(
                held, arrived.at[step - 1], sent.at[step], received.at[step], next_on(axis, step)
            )
            for step in range(1, count)
        ]
        for copy in copies:
            copy.wait()
        total = held[...]
        for step in range(1, count):
            total = total + arrived[step - 1]
        total_ref[...] = total
        held = total_ref
    out_ref[...] = held[...]


def sum_everywhere(values, axes, name):
    sizes = tuple((axis, lax.axis_size(axis)) for axis in axes)
    scratch = []
    for _, count in sizes:
        scratch.extend(
            [
                pltpu.VMEM(values.shape, jnp.float32),
                pltpu.VMEM((max(count - 1, 1), *values.shape), jnp.float32),
                pltpu.SemaphoreType.DMA((count,)),
                pltpu.SemaphoreType.DMA((count,)),
            ]
        )
    return call_kernel(
        functools.partial(sum_kernel, sizes),
        name,
        jax.ShapeDtypeStruct(values.shape, jnp.float32),
        scratch,
        (values,),
        8,
    )


def peer_pairs(count, step):
    if count & (count - 1) == 0:
        return [(i, i ^ step) for i in range(count)]
    return [((i + step) % count, i) for i in range(count)]


def replica_blocks(part):
    count = lax.axis_size("rep")
    me = lax.axis_index("rep")
    blocks = [part]
    for step in range(1, count):
        blocks.append(lax.ppermute(part, "rep", peer_pairs(count, step)))
    held = jnp.stack(blocks)
    places = []
    for index in range(count):
        if count & (count - 1) == 0:
            slot = lax.bitwise_xor(jnp.int32(index), me)
        else:
            slot = lax.rem(index - me + count, count)
        places.append(lax.dynamic_index_in_dim(held, slot, 0, keepdims=False))
    return places


def rolled(values, shift, dim):
    extent = values.shape[dim]
    return lax.dynamic_slice_in_dim(
        jnp.concatenate([values, values], axis=dim), shift, extent, axis=dim
    )


def gathered(weight):
    return lax.all_gather(weight, "shard", axis=0, tiled=True)


def scattered(grad, axes="shard"):
    return lax.psum_scatter(grad, axes, scatter_dimension=0, tiled=True)


def join_blocks(blocks, width):
    block = blocks[0].shape[-1]
    parts = []
    for index, part in enumerate(blocks):
        skip = max(index * block - (width - block), 0)
        if skip < block:
            parts.append(part[..., skip:])
    return jnp.concatenate(parts, axis=-1).astype(jnp.float32)


def body(
    x_in,
    query_key_value_weight,
    qkv_bias,
    output_weight,
    feedforward_entry_matrix,
    down_weight,
    norm_gains,
    piece_starts,
    seq_lengths,
    grad_out,
):
    seqs, span, width = x_in.shape
    shards = lax.axis_size("shard")
    place = lax.axis_index("shard")
    cores = lax.axis_size("tp")
    core = lax.axis_index("tp")
    reps = lax.axis_size("rep")
    length = span * shards
    half = span // cores
    rows = seqs * span
    own_rows = seqs * half
    depth = width // shards
    group_index = QUERY_HEADS // KEY_VALUE_HEADS
    joined_width = query_key_value_weight.shape[2]
    local_groups = joined_width // ((group_index + 2) * HEAD_SIZE)
    heads_width = output_weight.shape[2]
    hidden_width = down_weight.shape[2]
    block = -(-hidden_width // (reps * LANES)) * LANES
    first_owned = lax.axis_index("rep") * block
    first_unit = jnp.minimum(first_owned, hidden_width - block)
    owned = first_unit + jnp.arange(block, dtype=jnp.int32) >= first_owned
    root = math.sqrt(HEAD_SIZE)
    inner_pos = rolled(jnp.arange(span, dtype=jnp.int32), core * half, 0)
    own_pos = place * span + inner_pos
    all_pos = jnp.concatenate(
        [lax.rem(place + step, shards) * span + inner_pos for step in range(shards)]
    )
    cosine, sine = rope_tables(own_pos)
    cos_query = cosine[None, :, None, None, :]
    sin_query = sine[None, :, None, None, :]
    cos_key = cosine[None, :, None, :]
    sin_key = sine[None, :, None, :]
    own_ids = piece_ids(jnp.broadcast_to(own_pos, (seqs, span)), piece_starts)
    all_ids = piece_ids(jnp.broadcast_to(all_pos, (seqs, length)), piece_starts)
    same_piece = (own_ids[:, :, None] == all_ids[:, None, :]) & (own_ids[:, :, None] > 0)
    seen = (all_pos[None, None, :] < seq_lengths[:, None, None]) & (
        (all_pos[None, None, :] <= own_pos[None, :, None]) | same_piece
    )

    def own_block(weight):
        part = lax.dynamic_slice_in_dim(weight, first_unit, block, axis=weight.ndim - 1)
        return lax.optimization_barrier(jnp.where(owned, part, jnp.zeros_like(part)))

    def core_gather(values, name):
        tall = ring_gather(values, "tp", name, 6).reshape(cores, seqs, half, -1)
        return jnp.moveaxis(tall, 0, 1).reshape(rows, -1)

    def core_scatter(values):
        blocks = jnp.moveaxis(values.reshape(seqs, cores, half, -1), 1, 0)
        blocks = blocks.reshape(cores, own_rows, -1)
        return ring_scatter(blocks[1:].astype(jnp.bfloat16), blocks[0], "tp", 4, 8)

    gains_all = norm_gains.astype(jnp.float32)
    x_tall = rolled(x_in, core * half, 1).astype(jnp.float32)
    residual_state = x_tall[:, :half].reshape(own_rows, width)
    x_tall = x_tall.reshape(rows, width)
    first_normed = (x_tall * norm_scale(x_tall) * gains_all[0, 0]).astype(jnp.bfloat16)
    saved = []
    entry_blocks = own_block(feedforward_entry_matrix)
    down_blocks = own_block(down_weight)
    near_rows = reps * own_rows
    for index in range(LAYERS):
        full_both = weight_gather(
            jnp.concatenate([query_key_value_weight[index], output_weight[index]], axis=1)
        )
        full_qkv, full_out = full_both[:, :joined_width], full_both[:, joined_width:]
        part_entry = gathered(entry_blocks[index].reshape(depth, 2 * block))
        part_down = gathered(down_blocks[index])
        gains = gains_all[index]
        scale_one = norm_scale(residual_state)
        if index:
            first_normed = core_gather(
                (residual_state * scale_one * gains[0]).astype(jnp.bfloat16), 3
            )
        joined_output = product(first_normed, full_qkv) + qkv_bias[index].astype(jnp.float32)
        joined_output = joined_output.reshape(seqs, span, local_groups, group_index + 2, HEAD_SIZE)
        query_rows = rotate(joined_output[:, :, :, :group_index], cos_query, sin_query).astype(
            jnp.bfloat16
        )
        keys = rotate(joined_output[:, :, :, group_index], cos_key, sin_key).astype(jnp.bfloat16)
        content_entries = joined_output[:, :, :, group_index + 1].astype(jnp.bfloat16)
        pair = jnp.stack([keys, content_entries]).reshape(-1, HEAD_SIZE)
        pair_all = ring_gather(pair, "shard", 5, 12)
        pair_all = pair_all.reshape(shards, 2, seqs, span, local_groups, HEAD_SIZE)
        pair_all = jnp.moveaxis(pair_all, 0, 2).reshape(2, seqs, length, local_groups, HEAD_SIZE)
        keys_all, values_all = pair_all[0], pair_all[1]
        attention_logits = masked_scores(query_rows, keys_all, seen, root)
        log_total = jax.nn.logsumexp(attention_logits, axis=-1, keepdims=True)
        shares = jnp.exp(attention_logits - log_total).astype(jnp.bfloat16)
        mixed_output = jnp.einsum(
            "sgjqk,skgd->sqgjd", shares, values_all, preferred_element_type=jnp.float32
        )
        mixed_output = mixed_output.astype(jnp.bfloat16).reshape(rows, heads_width)
        middle_state = residual_state + core_scatter(right_product(mixed_output, full_out))
        scale_two = norm_scale(middle_state)
        plane_rows = plane_gather((middle_state * scale_two * gains[1]).astype(jnp.bfloat16))
        gate = product(plane_rows, part_entry[:, :block])
        upper = product(plane_rows, part_entry[:, block:])
        hidden_state = (jax.nn.silu(gate) * upper).astype(jnp.bfloat16)
        saved.append(
            (
                residual_state,
                scale_one,
                first_normed,
                query_rows,
                keys_all,
                values_all,
                log_total,
                mixed_output,
                middle_state,
                scale_two,
                plane_rows,
                gate,
                upper,
                hidden_state,
                full_qkv,
                full_out,
                part_entry,
                part_down,
            )
        )
        residual_state = middle_state + plane_scatter(
            right_product(hidden_state[near_rows:], part_down).astype(jnp.bfloat16),
            right_product(hidden_state[:near_rows], part_down),
        )
    out_own = residual_state.astype(jnp.bfloat16)
    grad_tall = rolled(grad_out, core * half, 1)[:, :half]
    flow = grad_tall.astype(jnp.float32).reshape(own_rows, width)
    up_pieces = [None] * LAYERS
    gate_pieces = [None] * LAYERS
    down_pieces = [None] * LAYERS
    qkv_pieces = [None] * LAYERS
    gain_grads = [None] * LAYERS
    bias_grads = [None] * LAYERS
    pending = None
    for index in reversed(range(LAYERS)):
        (
            residual_state,
            scale_one,
            first_normed,
            query_rows,
            keys_all,
            values_all,
            log_total,
            mixed_output,
            middle_state,
            scale_two,
            plane_rows,
            gate,
            upper,
            hidden_state,
            full_qkv,
            full_out,
            part_entry,
            part_down,
        ) = saved[index]
        gains = gains_all[index]
        plane_grad = plane_gather(flow.astype(jnp.bfloat16))
        hidden_grad = product(plane_grad, part_down)
        down_total = left_product(plane_grad, hidden_state)
        hidden_grad, down_total = lax.optimization_barrier((hidden_grad, down_total))
        down_own = scattered(down_total)
        sigmoid = jax.nn.sigmoid(gate)
        gate_grad = hidden_grad * upper * (sigmoid + gate * sigmoid * (1.0 - sigmoid))
        up_grad = hidden_grad * (gate * sigmoid)
        entry_grad = jnp.concatenate([gate_grad, up_grad], axis=1).astype(jnp.bfloat16)
        gate_total = left_product(plane_rows, entry_grad[:, :block])
        up_total = left_product(plane_rows, entry_grad[:, block:])
        entry_grad, gate_total, up_total = lax.optimization_barrier(
            (entry_grad, gate_total, up_total)
        )
        own_parts = (down_own, scattered(gate_total), scattered(up_total))
        far_product = right_product(entry_grad[near_rows:], part_entry).astype(jnp.bfloat16)
        near_product = right_product(entry_grad[:near_rows], part_entry)
        normed_two_grad = plane_scatter(far_product, near_product)
        middle_grad, gain_two = norm_back(middle_state, scale_two, gains[1], normed_two_grad)
        middle_grad = flow + middle_grad
        out_grad = core_gather(middle_grad.astype(jnp.bfloat16), 3)
        mixed_grad = product(out_grad, full_out).astype(jnp.bfloat16)
        mixed_grad, pending = lax.optimization_barrier((mixed_grad, pending))
        if pending is not None:
            down_pieces[index + 1], gate_pieces[index + 1], up_pieces[index + 1] = [
                replica_blocks(part) for part in pending
            ]
        pending = own_parts
        mixed_grad = mixed_grad.reshape(seqs, span, local_groups, group_index, HEAD_SIZE)
        attention_logits = masked_scores(query_rows, keys_all, seen, root)
        exact = jnp.exp(attention_logits - log_total)
        shares = exact.astype(jnp.bfloat16)
        share_grad = jnp.einsum(
            "sqgjd,skgd->sgjqk", mixed_grad, values_all, preferred_element_type=jnp.float32
        )
        centre = jnp.sum(exact * share_grad, axis=-1, keepdims=True)
        score_grad = (exact * (share_grad - centre)).astype(jnp.bfloat16)
        query_grad = (
            jnp.einsum(
                "sgjqk,skgd->sqgjd", score_grad, keys_all, preferred_element_type=jnp.float32
            )
            / root
        )
        key_grad = (
            jnp.einsum(
                "sgjqk,sqgjd->skgd", score_grad, query_rows, preferred_element_type=jnp.float32
            )
            / root
        )
        value_grad = jnp.einsum(
            "sgjqk,sqgjd->skgd", shares, mixed_grad, preferred_element_type=jnp.float32
        )
        pair = jnp.stack([key_grad, value_grad])
        pair = pair.reshape(2, seqs, shards, span, local_groups, HEAD_SIZE)
        pair = jnp.moveaxis(pair, 2, 0).reshape(shards, -1, HEAD_SIZE)
        pair_own = ring_scatter(pair[1:].astype(jnp.bfloat16), pair[0], "shard", 6, 14)
        pair_own = pair_own.reshape(2, seqs, span, local_groups, HEAD_SIZE)
        key_own, value_own = pair_own[0], pair_own[1]
        unrotated_asks = rotate_back(query_grad, cos_query, sin_query)
        key_raw = rotate_back(key_own, cos_key, sin_key)
        joined_grad = jnp.concatenate(
            [unrotated_asks, key_raw[:, :, :, None], value_own[:, :, :, None]], axis=3
        )
        joined_grad = joined_grad.reshape(rows, joined_width).astype(jnp.bfloat16)
        bias_grads[index] = jnp.sum(joined_grad, axis=0, dtype=jnp.float32)
        normed_one_grad = core_scatter(right_product(joined_grad, full_qkv))
        input_grad, gain_one = norm_back(residual_state, scale_one, gains[0], normed_one_grad)
        gain_grads[index] = jnp.stack([gain_one, gain_two])
        flow = middle_grad + input_grad
        both = jnp.concatenate(
            [left_product(first_normed, joined_grad), left_product(out_grad, mixed_output)], axis=1
        )
        if index:
            part = scattered(both, ("shard", "rep"))
            both_sum = jnp.concatenate(replica_blocks(part), axis=0)
        else:
            both_sum = gradient_sum(both)
        qkv_pieces[index] = both_sum.astype(jnp.float32)
    down_pieces[0], gate_pieces[0], up_pieces[0] = [replica_blocks(part) for part in pending]
    grad_gate_up = []
    for gates, ups in zip(gate_pieces, up_pieces):
        pairs = [
            lax.optimization_barrier(jnp.concatenate(pair, axis=1)).reshape(depth, 2, block)
            for pair in zip(gates, ups)
        ]
        grad_gate_up.append(join_blocks(pairs, hidden_width))
    grad_gate_up = jnp.stack(grad_gate_up)
    grad_down = jnp.stack([join_blocks(blocks, hidden_width) for blocks in down_pieces])
    grad_both = jnp.stack(qkv_pieces)
    grad_qkv = grad_both[:, :, :joined_width]
    grad_out_proj = grad_both[:, :, joined_width:]
    bias = jnp.stack(bias_grads)
    slots = jnp.arange(cores, dtype=jnp.int32)[:, None, None] == core
    bias_slots = jnp.where(slots, bias[None], 0.0)
    gains_own = jnp.stack(gain_grads)
    small = jnp.concatenate([gains_own.reshape(-1), bias_slots.reshape(-1)])
    small = sum_everywhere(small.reshape(-1, LANES), ("rep", "shard", "tp"), 7).reshape(-1)
    gains_total = small[: gains_own.size].reshape(gains_own.shape)
    bias_slots = small[gains_own.size :].reshape(bias_slots.shape)
    bias_total = lax.dynamic_index_in_dim(bias_slots, core, 0, keepdims=False)

    def whole_rows(values, name):
        tall = core_gather(values, name).reshape(seqs, span, width)
        return rolled(tall, lax.rem(cores - core, cores) * half, 1)

    return (
        whole_rows(out_own, 3),
        whole_rows(flow, 8),
        grad_qkv,
        bias_total,
        grad_out_proj,
        grad_gate_up,
        grad_down,
        gains_total,
    )


def solution(mesh):
    return jax.shard_map(
        body,
        mesh=mesh,
        in_specs=(
            P("rep", "shard", None),
            P(None, "shard", "tp"),
            P(None, "tp"),
            P(None, "shard", "tp"),
            P(None, "shard", None, "tp"),
            P(None, "shard", "tp"),
            P(),
            P("rep", None),
            P("rep"),
            P("rep", "shard", None),
        ),
        out_specs=(
            P("rep", "shard", None),
            P("rep", "shard", None),
            P(None, "shard", "tp"),
            P(None, "tp"),
            P(None, "shard", "tp"),
            P(None, "shard", None, "tp"),
            P(None, "shard", "tp"),
            P(),
        ),
        check_vma=False,
    )
```

profile of v0, /device:TPU:0, one launch (start us, length us, event | category | flops | bytes accessed | tf_op | source)
XLA Modules:
  0.0 1549.0 jit_solution(12493405595957543172)
XLA Ops:
  11.2 13.8 broadcast_select_fusion
  37.1 77.8 %shard_map.161 = bf16[4,4,96,1792]{3,2,1,0:T(8,128)(2,1)S(1)} custom-call(bf16[4,96,1792]{2,1,0:T(8,128)(2,1)S(1)} %pad_maximum_fusion.19.w_ref), custom_call_target="tpu_custom_call" | custom-call | bytes 150000000 | tf_op jit(solution)/shard_map/pallas_call | solution.py:131
  134.1 52.3 %shard_map.162 = bf16[4,768,128]{2,1,0:T(8,128)(2,1)S(1)} custom-call(bf16[768,128]{1,0:T(8,128)(2,1)S(1)} %bitcast.489), custom_call_target="tpu_custom_call" | custom-call | bytes 36000000 | tf_op jit(solution)/shard_map/pallas_call | solution.py:131
  205.7 31.5 %shard_map.164 = bf16[2,4,192,1536]{3,2,1,0:T(8,128)(2,1)S(1)} custom-call(bf16[192,1536]{1,0:T(8,128)(2,1)S(1)} %multiply_convert_fusion.9.x_ref), custom_call_target="tpu_custom_call" | custom-call | bytes 90000000 | tf_op jit(solution)/shard_map/pallas_call | solution.py:131
  239.6 73.4 %shard_map.167 = bf16[4,4,96,1792]{3,2,1,0:T(8,128)(2,1)S(1)} custom-call(bf16[4,96,1792]{2,1,0:T(8,128)(2,1)S(1)} %pad_maximum_fusion.20.w_ref), custom_call_target="tpu_custom_call" | custom-call | bytes 150000000 | tf_op jit(solution)/shard_map/pallas_call | solution.py:131
  315.8 30.8 %shard_map.173 = bf16[2,4,192,1536]{3,2,1,0:T(8,128)(2,1)S(1)} custom-call(bf16[192,1536]{1,0:T(8,128)(2,1)S(1)} %fusion.127.x_ref), custom_call_target="tpu_custom_call" | custom-call | bytes 90000000 | tf_op jit(solution)/shard_map/pallas_call | solution.py:131
  348.9 11.1 fusion.22
  360.0 9.0 fusion.20
  371.8 11.2 multiply_convert_fusion.5
  392.6 32.0 %shard_map.165 = f32[192,1536]{1,0:T(8,128)S(1)} custom-call(bf16[1,4,192,1536]{3,2,1,0:T(8,128)(2,1)S(1)} %bitcast.480, f32[4,192,1536]{2,1,0:T(8,128)S(1)} %bitcast.472), custom_call_target="tpu_custom_call" | custom-call | bytes 105000000 | tf_op jit(solution)/shard_map/pallas_call | solution.py:131
  431.9 45.5 %shard_map.168 = bf16[4,768,128]{2,1,0:T(8,128)(2,1)S(1)} custom-call(bf16[768,128]{1,0:T(8,128)(2,1)S(1)} %bitcast.490), custom_call_target="tpu_custom_call" | custom-call | bytes 36000000 | tf_op jit(solution)/shard_map/pallas_call | solution.py:131
  494.8 31.6 %shard_map.170 = bf16[2,4,192,1536]{3,2,1,0:T(8,128)(2,1)S(1)} custom-call(bf16[192,1536]{1,0:T(8,128)(2,1)S(1)} %multiply_convert_fusion.7.x_ref), custom_call_target="tpu_custom_call" | custom-call | bytes 90000000 | tf_op jit(solution)/shard_map/pallas_call | solution.py:131
  528.6 9.4 fusion.16
  538.0 13.8 multiply_convert_fusion.4
  551.8 9.9 convolution_convert_fusion.5
  561.7 8.1 copy.162
  569.8 10.6 multiply_convert_fusion.3
  582.3 7.8 convolution_convert_fusion.3
  590.1 10.5 convolution_convert_fusion.4
  616.9 31.8 %shard_map.171 = f32[192,1536]{1,0:T(8,128)S(1)} custom-call(bf16[1,4,192,1536]{3,2,1,0:T(8,128)(2,1)S(1)} %bitcast.477, f32[4,192,1536]{2,1,0:T(8,128)S(1)} %bitcast.469), custom_call_target="tpu_custom_call" | custom-call | bytes 105000000 | tf_op jit(solution)/shard_map/pallas_call | solution.py:131
  660.4 31.8 %shard_map.174 = f32[192,1536]{1,0:T(8,128)S(1)} custom-call(bf16[1,4,192,1536]{3,2,1,0:T(8,128)(2,1)S(1)} %bitcast.478, f32[4,192,1536]{2,1,0:T(8,128)S(1)} %bitcast.470), custom_call_target="tpu_custom_call" | custom-call | bytes 105000000 | tf_op jit(solution)/shard_map/pallas_call | solution.py:131
  701.9 9.8 fusion.3
  711.8 10.1 fusion.10
  738.7 39.8 %shard_map.176 = f32[768,128]{1,0:T(8,128)S(1)} custom-call(bf16[3,768,128]{2,1,0:T(8,128)(2,1)S(1)} %bitcast.476, f32[768,128]{1,0:T(8,128)S(1)} %bitcast.482), custom_call_target="tpu_custom_call" | custom-call | bytes 42000000 | tf_op jit(solution)/shard_map/pallas_call | solution.py:131
  795.6 31.6 %shard_map.178 = bf16[2,4,192,1536]{3,2,1,0:T(8,128)(2,1)S(1)} custom-call(bf16[192,1536]{1,0:T(8,128)(2,1)S(1)} %get-tuple-element.86.x_ref), custom_call_target="tpu_custom_call" | custom-call | bytes 90000000 | tf_op jit(solution)/shard_map/pallas_call | solution.py:131
  829.3 8.0 convolution_convert_fusion.2
  837.4 10.9 fusion.28
  848.3 8.1 copy.177
  856.4 11.1 multiply_convert_fusion.1
  874.0 9.8 convolution_convert_fusion
  883.8 10.5 convolution_convert_fusion.1
  896.9 9.2 fusion.34
  906.2 9.0 fusion.45
  915.3 31.8 %shard_map.179 = f32[192,1536]{1,0:T(8,128)S(1)} custom-call(bf16[1,4,192,1536]{3,2,1,0:T(8,128)(2,1)S(1)} %bitcast.479, f32[4,192,1536]{2,1,0:T(8,128)S(1)} %bitcast.471), custom_call_target="tpu_custom_call" | custom-call | bytes 105000000 | tf_op jit(solution)/shard_map/pallas_call | solution.py:131
  957.5 8.8 copy.218
  979.1 13.2 fusion
  1013.8 42.6 %shard_map.181 = f32[768,128]{1,0:T(8,128)S(1)} custom-call(bf16[3,768,128]{2,1,0:T(8,128)(2,1)S(1)} %bitcast.475, f32[768,128]{1,0:T(8,128)S(1)} %bitcast.481), custom_call_target="tpu_custom_call" | custom-call | bytes 42000000 | tf_op jit(solution)/shard_map/pallas_call | solution.py:131
  1081.3 40.7 %shard_map.185 = f32[80,128]{1,0:T(8,128)S(1)} custom-call(f32[80,128]{1,0:T(8,128)S(1)} %maximum_bitcast_fusion.2.x_ref), custom_call_target="tpu_custom_call" | custom-call | bytes 24000000 | tf_op jit(solution)/shard_map/pallas_call | solution.py:131
  1132.7 8.3 copy.190
  1143.6 157.9 %shard_map.184 = bf16[4,96,1792]{2,1,0:T(8,128)(2,1)S(1)} custom-call(bf16[4,4,96,1792]{3,2,1,0:T(8,128)(2,1)S(1)} %bitcast.431), custom_call_target="tpu_custom_call" | custom-call | bytes 270000000 | tf_op jit(solution)/shard_map/pallas_call | solution.py:131
  1320.7 32.3 %collective-permute-done.15 = bf16[384,1152]{1,0:T(8,128)(2,1)S(1)} collective-permute-done((bf16[384,1152]{1,0:T(8,128)(2,1)}, bf16[384,1152]{1,0:T(8,128)(2,1)S(1)}, u32[]{:S(2)}, u32[]{:S(2)}) %collective-permute-start.15) | collective-permute-done | bytes 884768 | tf_op jit(solution)/shard_map/ppermute | solution.py:588
  1355.8 39.6 %collective-permute-done.16 = bf16[384,1152]{1,0:T(8,128)(2,1)S(1)} collective-permute-done((bf16[384,1152]{1,0:T(8,128)(2,1)}, bf16[384,1152]{1,0:T(8,128)(2,1)S(1)}, u32[]{:S(2)}, u32[]{:S(2)}) %collective-permute-start.16) | collective-permute-done | bytes 884768 | tf_op jit(solution)/shard_map/ppermute | solution.py:588
  1424.4 14.3 collective-permute-done.10
  1442.2 14.0 collective-permute-done.12
  1456.3 18.9 %collective-permute-done.13 = bf16[384,1152]{1,0:T(8,128)(2,1)} collective-permute-done((bf16[384,1152]{1,0:T(8,128)(2,1)}, bf16[384,1152]{1,0:T(8,128)(2,1)}, u32[]{:S(2)}, u32[]{:S(2)}) %collective-permute-start.13) | collective-permute-done | bytes 884768 | tf_op jit(solution)/shard_map/ppermute | solution.py:588
  1492.2 15.4 maximum_convert_fusion
  1512.5 7.6 maximum_convert_fusion.1
  1522.4 7.9 collective-permute-done.1
  (592 shorter events, 356.5 us)
Async XLA Ops:
  7.2 341.7 %all-gather.13.cloned.1.call-start = ((), (), s32[]{:S(2)}) async-start(), calls=%async_computation.16 | async-start | bytes 4423680 | tf_op jit(solution)/shard_map/all_gather | solution.py:608
  11.2 348.8 %all-gather.7.cloned.1.call-start = ((), (), s32[]{:S(2)}) async-start(), calls=%async_computation.7 | async-start | bytes 8847360 | tf_op jit(solution)/shard_map/all_gather | solution.py:608
  29.2 353.8 %all-gather.11.cloned.1.call-start = ((), (), s32[]{:S(2)}) async-start(), calls=%async_computation.15 | async-start | bytes 4423680 | tf_op jit(solution)/shard_map/all_gather | solution.py:608
  29.9 498.6 %all-gather.9.cloned.1.call-start = ((), (), s32[]{:S(2)}) async-start(), calls=%async_computation.8 | async-start | bytes 8847360 | tf_op jit(solution)/shard_map/all_gather | solution.py:608
  31.4 947.3 %reduce-scatter.12.cloned.1.call-start = ((), (), s32[]{:S(2)}) async-start(), calls=%async_computation.10 | async-start | bytes 4423680 | tf_op jit(solution)/shard_map/reduce_scatter | solution.py:612
  34.0 81.5 %copy-start.43 = (bf16[1,384,1536]{2,1,0:T(8,128)(2,1)}, bf16[1,384,1536]{2,1,0:T(8,128)(2,1)S(1)}, u32[]{:S(2)}) copy-start(bf16[1,384,1536]{2,1,0:T(8,128)(2,1)S(1)} %get-tuple-element.97) | copy-start | bytes 3538948
  34.4 81.1 %copy-start.114 = (f32[384]{0:T(512)}, f32[384]{0:T(512)S(1)}, u32[]{:S(2)}) copy-start(f32[384]{0:T(512)S(1)} %add_rsqrt_fusion) | copy-start | bytes 4612
  35.0 80.5 %copy-start.90 = (f32[1536]{0:T(1024)}, f32[1536]{0:T(1024)S(1)}, u32[]{:S(2)}) copy-start(f32[1536]{0:T(1024)S(1)} %get-tuple-element.79) | copy-start | bytes 18436
  35.0 170.5 %copy-start.85 = (f32[1536]{0:T(1024)}, f32[1536]{0:T(1024)S(1)}, u32[]{:S(2)}) copy-start(f32[1536]{0:T(1024)S(1)} %get-tuple-element.78) | copy-start | bytes 18436
  35.0 390.4 %copy-start.87 = (f32[1536]{0:T(1024)}, f32[1536]{0:T(1024)S(1)}, u32[]{:S(2)}) copy-start(f32[1536]{0:T(1024)S(1)} %get-tuple-element.77) | copy-start | bytes 18436
  37.0 77.8 %copy-start.100 = (bf16[2,1024]{1,0:T(2,128)(2,1)S(1)}, bf16[2,1024]{1,0:T(2,128)(2,1)}, u32[]{:S(2)}) copy-start(bf16[2,1024]{1,0:T(2,128)(2,1)} %param.12) | copy-start | bytes 12292
  120.7 65.6 %copy-start.66 = (f32[1,1,384,1,64]{4,2,3,1,0:T(8,128)}, f32[1,1,384,1,64]{4,2,3,1,0:T(8,128)S(1)}, u32[]{:S(2)}) copy-start(f32[1,1,384,1,64]{4,2,3,1,0:T(8,128)S(1)} %get-tuple-element.180) | copy-start | bytes 294916
  132.3 54.2 %copy-start.99 = (s32[384]{0:T(512)S(1)}, s32[384]{0:T(512)}, u32[]{:S(2)}) copy-start(s32[384]{0:T(512)} %copy-done.98) | copy-start | bytes 4612
  132.3 54.2 %copy-start.108 = (pred[1536]{0:T(1024)(128)(4,1)S(1)}, pred[1536]{0:T(1024)(128)(4,1)}, u32[]{:S(2)}) copy-start(pred[1536]{0:T(1024)(128)(4,1)} %broadcast_compare_fusion) | copy-start | bytes 4612
  132.3 54.2 %copy-start.116 = (pred[384]{0:T(512)(128)(4,1)S(1)}, pred[384]{0:T(512)(128)(4,1)}, u32[]{:S(2)}) copy-start(pred[384]{0:T(512)(128)(4,1)} %broadcast_compare_fusion.1) | copy-start | bytes 1156
  132.3 56.1 %copy-start.62 = (f32[384,128]{0,1:T(8,128)S(1)}, f32[384,128]{0,1:T(8,128)}, u32[]{:S(2)}) copy-start(f32[384,128]{0,1:T(8,128)} %copy.152) | copy-start | bytes 589828
  132.3 56.1 %copy-start.64 = (f32[384,128]{0,1:T(8,128)S(1)}, f32[384,128]{0,1:T(8,128)}, u32[]{:S(2)}) copy-start(f32[384,128]{0,1:T(8,128)} %copy.153) | copy-start | bytes 589828
  204.9 219.7 %copy-start.16 = (f32[192,1536]{1,0:T(8,128)}, f32[192,1536]{1,0:T(8,128)S(1)}, u32[]{:S(2)}) copy-start(f32[192,1536]{1,0:T(8,128)S(1)} %get-tuple-element.95) | copy-start | bytes 3538948
  239.6 75.8 %copy-start.41 = (bf16[1,384,1536]{2,1,0:T(8,128)(2,1)S(1)}, bf16[1,384,1536]{2,1,0:T(8,128)(2,1)}, u32[]{:S(2)}) copy-start(bf16[1,384,1536]{2,1,0:T(8,128)(2,1)} %param.19) | copy-start | bytes 3538948
  607.1 371.6 %reduce-scatter.14.cloned.1.call-start = ((), (), s32[]{:S(2)}) async-start(), calls=%async_computation.11 | async-start | bytes 4423680 | tf_op jit(solution)/shard_map/reduce_scatter | solution.py:612
  711.7 267.0 %reduce-scatter.10.cloned.1.call-start = ((), (), s32[]{:S(2)}) async-start(), calls=%async_computation.9 | async-start | bytes 4423680 | tf_op jit(solution)/shard_map/reduce_scatter | solution.py:612
  837.3 241.9 %reduce-scatter.16.cloned.1.call-start = ((), (), s32[]{:S(2)}) async-start(), calls=%async_computation.12 | async-start | bytes 4423680 | tf_op jit(solution)/shard_map/reduce_scatter | solution.py:612
  894.4 231.5 %reduce-scatter.18.cloned.1.call-start = ((), (), s32[]{:S(2)}) async-start(), calls=%async_computation.13 | async-start | bytes 4423680 | tf_op jit(solution)/shard_map/reduce_scatter | solution.py:612
  895.1 418.9 %reduce-scatter.20.cloned.1.call-start = ((), (), s32[]{:S(2)}) async-start(), calls=%async_computation.14 | async-start | bytes 4423680 | tf_op jit(solution)/shard_map/reduce_scatter | solution.py:612
  895.7 612.0 %reduce-scatter.22.cloned.1.call-start = ((), (), s32[]{:S(2)}) async-start(), calls=%async_computation.17 | async-start | bytes 5849088
  1079.2 50.4 %collective-permute-start.3 = (bf16[384,1152]{1,0:T(8,128)(2,1)}, bf16[384,1152]{1,0:T(8,128)(2,1)S(1)}, u32[]{:S(2)}, u32[]{:S(2)}) collective-permute-start(bf16[384,1152]{1,0:T(8,128)(2,1)} %reduce-scatter.16.cloned.1.call-done), channel_id=1, source_target_pairs={{0,8},{8,0},{16,24},{24,16},{1,9},{9,1},{17,25},{25,17},{2,10},{10... | collective-permute-start | bytes 2654216 | tf_op jit(solution)/shard_map/ppermute | solution.py:588
  1122.1 186.7 %collective-permute-start.4 = (bf16[384,1152]{1,0:T(8,128)(2,1)}, bf16[384,1152]{1,0:T(8,128)(2,1)}, u32[]{:S(2)}, u32[]{:S(2)}) collective-permute-start(bf16[384,1152]{1,0:T(8,128)(2,1)} %reduce-scatter.16.cloned.1.call-done), channel_id=1, source_target_pairs={{0,16},{8,24},{16,0},{24,8},{1,17},{9,25},{17,1},{25,9},{2,18},{10... | collective-permute-start | bytes 2654216 | tf_op jit(solution)/shard_map/ppermute | solution.py:588
  1123.4 186.8 %collective-permute-start.5 = (bf16[384,1152]{1,0:T(8,128)(2,1)}, bf16[384,1152]{1,0:T(8,128)(2,1)}, u32[]{:S(2)}, u32[]{:S(2)}) collective-permute-start(bf16[384,1152]{1,0:T(8,128)(2,1)} %reduce-scatter.16.cloned.1.call-done), channel_id=1, source_target_pairs={{0,24},{8,16},{16,8},{24,0},{1,25},{9,17},{17,9},{25,1},{2,26},{10... | collective-permute-start | bytes 2654216 | tf_op jit(solution)/shard_map/ppermute | solution.py:588
  1125.9 188.1 %collective-permute-start.6 = (bf16[384,1152]{1,0:T(8,128)(2,1)}, bf16[384,1152]{1,0:T(8,128)(2,1)}, u32[]{:S(2)}, u32[]{:S(2)}) collective-permute-start(bf16[384,1152]{1,0:T(8,128)(2,1)} %reduce-scatter.18.cloned.1.call-done), channel_id=1, source_target_pairs={{0,8},{8,0},{16,24},{24,16},{1,9},{9,1},{17,25},{25,17},{2,10},{10... | collective-permute-start | bytes 2654216 | tf_op jit(solution)/shard_map/ppermute | solution.py:588
  1125.9 188.3 %collective-permute-start.7 = (bf16[384,1152]{1,0:T(8,128)(2,1)}, bf16[384,1152]{1,0:T(8,128)(2,1)}, u32[]{:S(2)}, u32[]{:S(2)}) collective-permute-start(bf16[384,1152]{1,0:T(8,128)(2,1)} %reduce-scatter.18.cloned.1.call-done), channel_id=1, source_target_pairs={{0,16},{8,24},{16,0},{24,8},{1,17},{9,25},{17,1},{25,9},{2,18},{10... | collective-permute-start | bytes 2654216 | tf_op jit(solution)/shard_map/ppermute | solution.py:588
  1129.6 185.1 %collective-permute-start.8 = (bf16[384,1152]{1,0:T(8,128)(2,1)}, bf16[384,1152]{1,0:T(8,128)(2,1)}, u32[]{:S(2)}, u32[]{:S(2)}) collective-permute-start(bf16[384,1152]{1,0:T(8,128)(2,1)} %reduce-scatter.18.cloned.1.call-done), channel_id=1, source_target_pairs={{0,24},{8,16},{16,8},{24,0},{1,25},{9,17},{17,9},{25,1},{2,26},{10... | collective-permute-start | bytes 2654216 | tf_op jit(solution)/shard_map/ppermute | solution.py:588
  1143.6 159.5 %slice-start.14 = ((f32[80,128]{1,0:T(8,128)}), f32[48,128]{1,0:T(8,128)S(1)}, s32[]{:S(2)}) async-start(f32[80,128]{1,0:T(8,128)} %copy-done.12), calls=%async_computation.32 | async-start | bytes 49152 | tf_op jit(solution)/shard_map/slice | solution.py:890
  1308.8 94.1 %collective-permute-start.18 = (bf16[384,1152]{1,0:T(8,128)(2,1)}, bf16[384,1152]{1,0:T(8,128)(2,1)}, u32[]{:S(2)}, u32[]{:S(2)}) collective-permute-start(bf16[384,1152]{1,0:T(8,128)(2,1)} %reduce-scatter.10.cloned.1.call-done), channel_id=1, source_target_pairs={{0,8},{8,0},{16,24},{24,16},{1,9},{9,1},{17,25},{25,17},{2,10},{10... | collective-permute-start | bytes 2654216 | tf_op jit(solution)/shard_map/ppermute | solution.py:588
  1310.3 94.1 %collective-permute-start.19 = (bf16[384,1152]{1,0:T(8,128)(2,1)}, bf16[384,1152]{1,0:T(8,128)(2,1)}, u32[]{:S(2)}, u32[]{:S(2)}) collective-permute-start(bf16[384,1152]{1,0:T(8,128)(2,1)} %reduce-scatter.10.cloned.1.call-done), channel_id=1, source_target_pairs={{0,16},{8,24},{16,0},{24,8},{1,17},{9,25},{17,1},{25,9},{2,18},{10... | collective-permute-start | bytes 2654216 | tf_op jit(solution)/shard_map/ppermute | solution.py:588
  1314.0 39.0 %collective-permute-start.15 = (bf16[384,1152]{1,0:T(8,128)(2,1)}, bf16[384,1152]{1,0:T(8,128)(2,1)S(1)}, u32[]{:S(2)}, u32[]{:S(2)}) collective-permute-start(bf16[384,1152]{1,0:T(8,128)(2,1)} %reduce-scatter.20.cloned.1.call-done), channel_id=1, source_target_pairs={{0,8},{8,0},{16,24},{24,16},{1,9},{9,1},{17,25},{25,17},{2,10},{10... | collective-permute-start | bytes 2654216 | tf_op jit(solution)/shard_map/ppermute | solution.py:588
  1314.2 81.3 %collective-permute-start.16 = (bf16[384,1152]{1,0:T(8,128)(2,1)}, bf16[384,1152]{1,0:T(8,128)(2,1)S(1)}, u32[]{:S(2)}, u32[]{:S(2)}) collective-permute-start(bf16[384,1152]{1,0:T(8,128)(2,1)} %reduce-scatter.20.cloned.1.call-done), channel_id=1, source_target_pairs={{0,16},{8,24},{16,0},{24,8},{1,17},{9,25},{17,1},{25,9},{2,18},{10... | collective-permute-start | bytes 2654216 | tf_op jit(solution)/shard_map/ppermute | solution.py:588
  1314.7 82.2 %collective-permute-start.17 = (bf16[384,1152]{1,0:T(8,128)(2,1)}, bf16[384,1152]{1,0:T(8,128)(2,1)S(1)}, u32[]{:S(2)}, u32[]{:S(2)}) collective-permute-start(bf16[384,1152]{1,0:T(8,128)(2,1)} %reduce-scatter.20.cloned.1.call-done), channel_id=1, source_target_pairs={{0,24},{8,16},{16,8},{24,0},{1,25},{9,17},{17,9},{25,1},{2,26},{10... | collective-permute-start | bytes 2654216 | tf_op jit(solution)/shard_map/ppermute | solution.py:588
  1320.4 77.1 %copy-start.71 = (bf16[384,1152]{1,0:T(8,128)(2,1)S(1)}, bf16[384,1152]{1,0:T(8,128)(2,1)}, u32[]{:S(2)}) copy-start(bf16[384,1152]{1,0:T(8,128)(2,1)} %reduce-scatter.20.cloned.1.call-done) | copy-start | bytes 2654212
  1353.0 52.9 %collective-permute-start.20 = (bf16[384,1152]{1,0:T(8,128)(2,1)}, bf16[384,1152]{1,0:T(8,128)(2,1)S(1)}, u32[]{:S(2)}, u32[]{:S(2)}) collective-permute-start(bf16[384,1152]{1,0:T(8,128)(2,1)} %reduce-scatter.10.cloned.1.call-done), channel_id=1, source_target_pairs={{0,24},{8,16},{16,8},{24,0},{1,25},{9,17},{17,9},{25,1},{2,26},{10... | collective-permute-start | bytes 2654216 | tf_op jit(solution)/shard_map/ppermute | solution.py:588
  1395.5 27.5 %collective-permute-start.9 = (bf16[384,1152]{1,0:T(8,128)(2,1)}, bf16[384,1152]{1,0:T(8,128)(2,1)}, u32[]{:S(2)}, u32[]{:S(2)}) collective-permute-start(bf16[384,1152]{1,0:T(8,128)(2,1)} %reduce-scatter.12.cloned.1.call-done), channel_id=1, source_target_pairs={{0,8},{8,0},{16,24},{24,16},{1,9},{9,1},{17,25},{25,17},{2,10},{10... | collective-permute-start | bytes 2654216 | tf_op jit(solution)/shard_map/ppermute | solution.py:588
  1396.9 41.8 %collective-permute-start.10 = (bf16[384,1152]{1,0:T(8,128)(2,1)}, bf16[384,1152]{1,0:T(8,128)(2,1)}, u32[]{:S(2)}, u32[]{:S(2)}) collective-permute-start(bf16[384,1152]{1,0:T(8,128)(2,1)} %reduce-scatter.12.cloned.1.call-done), channel_id=1, source_target_pairs={{0,16},{8,24},{16,0},{24,8},{1,17},{9,25},{17,1},{25,9},{2,18},{10... | collective-permute-start | bytes 2654216 | tf_op jit(solution)/shard_map/ppermute | solution.py:588
  1402.9 35.8 %collective-permute-start.11 = (bf16[384,1152]{1,0:T(8,128)(2,1)}, bf16[384,1152]{1,0:T(8,128)(2,1)}, u32[]{:S(2)}, u32[]{:S(2)}) collective-permute-start(bf16[384,1152]{1,0:T(8,128)(2,1)} %reduce-scatter.12.cloned.1.call-done), channel_id=1, source_target_pairs={{0,24},{8,16},{16,8},{24,0},{1,25},{9,17},{17,9},{25,1},{2,26},{10... | collective-permute-start | bytes 2654216 | tf_op jit(solution)/shard_map/ppermute | solution.py:588
  1404.4 51.9 %collective-permute-start.12 = (bf16[384,1152]{1,0:T(8,128)(2,1)}, bf16[384,1152]{1,0:T(8,128)(2,1)}, u32[]{:S(2)}, u32[]{:S(2)}) collective-permute-start(bf16[384,1152]{1,0:T(8,128)(2,1)} %reduce-scatter.14.cloned.1.call-done), channel_id=1, source_target_pairs={{0,8},{8,0},{16,24},{24,16},{1,9},{9,1},{17,25},{25,17},{2,10},{10... | collective-permute-start | bytes 2654216 | tf_op jit(solution)/shard_map/ppermute | solution.py:588
  1405.8 69.4 %collective-permute-start.13 = (bf16[384,1152]{1,0:T(8,128)(2,1)}, bf16[384,1152]{1,0:T(8,128)(2,1)}, u32[]{:S(2)}, u32[]{:S(2)}) collective-permute-start(bf16[384,1152]{1,0:T(8,128)(2,1)} %reduce-scatter.14.cloned.1.call-done), channel_id=1, source_target_pairs={{0,16},{8,24},{16,0},{24,8},{1,17},{9,25},{17,1},{25,9},{2,18},{10... | collective-permute-start | bytes 2654216 | tf_op jit(solution)/shard_map/ppermute | solution.py:588
  1422.9 52.3 %collective-permute-start.14 = (bf16[384,1152]{1,0:T(8,128)(2,1)}, bf16[384,1152]{1,0:T(8,128)(2,1)S(1)}, u32[]{:S(2)}, u32[]{:S(2)}) collective-permute-start(bf16[384,1152]{1,0:T(8,128)(2,1)} %reduce-scatter.14.cloned.1.call-done), channel_id=1, source_target_pairs={{0,24},{8,16},{16,8},{24,0},{1,25},{9,17},{17,9},{25,1},{2,26},{10... | collective-permute-start | bytes 2654216 | tf_op jit(solution)/shard_map/ppermute | solution.py:588
  1508.9 13.5 collective-permute-start
  1509.6 20.7 %collective-permute-start.1 = (bf16[96,1792]{0,1:T(8,128)(2,1)S(1)}, bf16[96,1792]{0,1:T(8,128)(2,1)S(1)}, u32[]{:S(2)}, u32[]{:S(2)}) collective-permute-start(bf16[96,1792]{0,1:T(8,128)(2,1)S(1)} %copy.219), channel_id=1, source_target_pairs={{0,16},{8,24},{16,0},{24,8},{1,17},{9,25},{17,1},{25,9},{2,18},{10... | collective-permute-start | bytes 1032200 | tf_op jit(solution)/shard_map/ppermute | solution.py:588
  1510.7 19.7 %collective-permute-start.2 = (bf16[96,1792]{0,1:T(8,128)(2,1)S(1)}, bf16[96,1792]{0,1:T(8,128)(2,1)S(1)}, u32[]{:S(2)}, u32[]{:S(2)}) collective-permute-start(bf16[96,1792]{0,1:T(8,128)(2,1)S(1)} %copy.219), channel_id=1, source_target_pairs={{0,24},{8,16},{16,8},{24,0},{1,25},{9,17},{17,9},{25,1},{2,26},{10... | collective-permute-start | bytes 1032200 | tf_op jit(solution)/shard_map/ppermute | solution.py:588
  (130 other events, 1658.9 us)
Sparse Core Ops, SparseCore 0:
  11.3 101.7 all-gather.12
  115.2 143.3 all-gather.6
  260.7 85.2 all-gather.10
  348.0 143.2 all-gather.8
  607.2 75.2 reduce-scatter.11
  711.8 88.5 reduce-scatter.13
  837.4 77.9 reduce-scatter.9
  917.7 66.6 reduce-scatter.15
  986.8 79.2 reduce-scatter.17
  1068.2 72.0 reduce-scatter.19
  1145.6 209.0 reduce-scatter.21
where the time goes:
time: 1560 us; the launch traced here: 1550 us
  Pallas kernels  803 us (51%)
  matrix products  255 us (16%)
  other arithmetic  174 us (11%)
  local copies, waits for them, and re-layouts  138 us (9%)
  waiting for transfers between devices  132 us (8%)
  starting transfers between devices  29.5 us (2%)
  between operations  17.5 us (1%)
    pallas_call x25, Pallas kernels, call_kernel(): pl.pallas_call(kernel, out_shape=out_shape, in_specs=[pl.BlockSpec(memory...  803 us
    ppermute x21, waiting for transfers between devices, replica_blocks(): blocks.append(lax.ppermute(part, 'rep', peer_pairs(count, step)))  129 us
    dot_general x10, matrix products, product(): return jnp.dot(left, right, preferred_element_type=jnp.float32)  75.4 us
    dot_general x10, matrix products, left_product(): lax.dot_general(left, right, (((0,), (0,)), ((), ())), preferred_element_...  67 us
    dot_general x12, matrix products, right_product(): lax.dot_general(left, right, (((1,), (1,)), ((), ())), preferred_element_...  58 us
    unnamed x299, local copies, waits for them, and re-layouts  55.5 us
  transfers between devices with their start and end apart: 32, of which 7 were waited for; matrix products, arithmetic and copies ran while one was open for 28% of the time, Pallas kernels for 52%

commit v1 on v0

--- a/solution.py
+++ b/solution.py
@@ -102,6 +102,22 @@
                 barrier, inc=1, device_id=next_on(axis, step), device_id_type=MESH
             )
     pl.semaphore_wait(barrier, sum(count - 1 for _, count in sizes))
+
+
+def greet_devices(devices):
+    barrier = pltpu.get_barrier_semaphore()
+    for device in devices:
+        pl.semaphore_signal(barrier, inc=1, device_id=device, device_id_type=MESH)
+    pl.semaphore_wait(barrier, len(devices))
+
+
+def square_peers():
+    me = lax.axis_index("rep")
+    return me, me + 1 - 2 * lax.rem(me, 2), lax.rem(me + 2, 4)
+
+
+def slot_of(peer, me):
+    return lax.rem(peer - me + 4, 4)
 
 
 def start_copy(source, target, sent, received, device):
@@ -117,11 +133,11 @@
     return copy
 
 
-def by_rows(rows, update):
+def by_rows(rows, update, base=0):
     size = next((size for size in (32, 16) if rows % size == 0), rows)
 
     def step(index, carry):
-        update(pl.ds(pl.multiple_of(index * size, size), size))
+        update(pl.ds(pl.multiple_of(base + index * size, 16), size))
         return carry
 
     lax.fori_loop(0, rows // size, step, 0)
@@ -253,10 +269,75 @@
         copy.wait()
 
 
+def square_gather_kernel(cores, x_ref, out_ref, sent, received, sent_on, received_on):
+    me, beside, above = square_peers()
+    ways = {"beside": {"rep": beside}, "above": {"rep": above}}
+    greet_devices(list(ways.values()) + [next_on("tp", step) for step in range(1, cores)])
+    half = x_ref.shape[0] // 2
+    low, high = pl.ds(0, half), pl.ds(half, half)
+    by_side = start_copy(
+        x_ref, out_ref.at[0, slot_of(me, beside)], sent.at[0], received.at[0], ways["beside"]
+    )
+    by_top = start_copy(
+        x_ref, out_ref.at[0, slot_of(me, above)], sent.at[1], received.at[1], ways["above"]
+    )
+    passed = []
+
+    def pass_on(source, slot, role):
+        for step in range(1, cores):
+            passed.append(
+                start_copy(
+                    source,
+                    out_ref.at[cores - step, slot],
+                    sent_on.at[step, role],
+                    received_on.at[cores - step, role],
+                    next_on("tp", step),
+                )
+            )
+
+    pass_on(x_ref, 0, 0)
+    out_ref[0, 0] = x_ref[...]
+    side_slot, top_slot = slot_of(beside, me), slot_of(above, me)
+    by_side.wait_recv()
+    upward = start_copy(
+        out_ref.at[0, side_slot, low],
+        out_ref.at[0, slot_of(beside, above), low],
+        sent.at[2],
+        received.at[2],
+        ways["above"],
+    )
+    pass_on(out_ref.at[0, side_slot], side_slot, 1)
+    by_top.wait_recv()
+    sideward = start_copy(
+        out_ref.at[0, top_slot, high],
+        out_ref.at[0, slot_of(above, beside), high],
+        sent.at[3],
+        received.at[3],
+        ways["beside"],
+    )
+    pass_on(out_ref.at[0, top_slot], top_slot, 2)
+    upward.wait_recv()
+    sideward.wait_recv()
+    far_slot = 4 - side_slot
+    pass_on(out_ref.at[0, far_slot], far_slot, 3)
+    for copy in (by_side, by_top, upward, sideward):
+        copy.wait_send()
+    for copy in passed:
+        copy.wait()
+
+
+def in_square(reps, rows):
+    return reps == 4 and rows % 32 == 0
+
+
 def plane_gather(rows):
     reps, cores = lax.axis_size("rep"), lax.axis_size("tp")
     gathered = call_kernel(
-        functools.partial(plane_gather_kernel, reps, cores),
+        (
+            functools.partial(square_gather_kernel, cores)
+            if in_square(reps, rows.shape[0])
+            else functools.partial(plane_gather_kernel, reps, cores)
+        ),
         1,
         jax.ShapeDtypeStruct((cores, reps, *rows.shape), rows.dtype),
         [
@@ -338,11 +419,120 @@
     by_rows(rows, finish)
 
 
+def square_scatter_kernel(
+    cores,
+    far_ref,
+    near_ref,
+    out_ref,
+    arrived,
+    staged,
+    landed,
+    crossed,
+    sent,
+    received,
+    sent_on,
+    received_on,
+):
+    me, beside, above = square_peers()
+    ways = {"beside": {"rep": beside}, "above": {"rep": above}}
+    greet_devices(list(ways.values()) + [next_on("tp", step) for step in range(1, cores)])
+    half = near_ref.shape[1] // 2
+    low, high = pl.ds(0, half), pl.ds(half, half)
+    side_slot, top_slot = slot_of(beside, me), slot_of(above, me)
+    slots = (4 - side_slot, side_slot, top_slot, 0)
+    first = {}
+    for role, slot in enumerate(slots):
+        for step in range(1, cores):
+            first[role, step] = start_copy(
+                far_ref.at[step - 1, slot],
+                arrived.at[step - 1, role],
+                sent.at[step, role],
+                received.at[step, role],
+                next_on("tp", step),
+            )
+
+    def near_sum(role, some):
+        total = near_ref[slots[role], some, :]
+        for step in range(1, cores):
+            total = total + arrived[step - 1, role, some, :].astype(jnp.float32)
+        return total
+
+    def await_role(role):
+        for step in range(1, cores):
+            first[role, step].wait_recv()
+
+    def stage(role, base, extra=None):
+        def fill(some):
+            total = near_sum(role, some)
+            if extra is not None:
+                inner = pl.ds(some.start - base, some.size)
+                total = total + crossed[extra, inner, :].astype(jnp.float32)
+            staged[role, some, :] = total.astype(jnp.bfloat16)
+
+        by_rows(half, fill, base)
+
+    def send(role, rows, target, index, way):
+        return start_copy(
+            staged.at[role, rows], target, sent_on.at[index], received_on.at[index], ways[way]
+        )
+
+    await_role(0)
+    stage(0, 0)
+    corner_low = send(0, low, crossed.at[0], 0, "beside")
+    stage(0, half)
+    corner_high = send(0, high, crossed.at[1], 1, "above")
+    await_role(1)
+    stage(1, 0)
+    side_low = send(1, low, landed.at[0, low], 2, "beside")
+    await_role(2)
+    stage(2, half)
+    top_high = send(2, high, landed.at[1, high], 3, "above")
+    corner_low.wait_recv()
+    stage(2, 0, 0)
+    top_low = send(2, low, landed.at[1, low], 4, "above")
+    corner_high.wait_recv()
+    stage(1, half, 1)
+    side_high = send(1, high, landed.at[0, high], 5, "beside")
+    await_role(3)
+    for copy in (side_low, top_high, top_low, side_high):
+        copy.wait_recv()
+
+    def finish(some):
+        total = near_sum(3, some)
+        for way in range(2):
+            total = total + landed[way, some, :].astype(jnp.float32)
+        out_ref[some, :] = total
+
+    by_rows(near_ref.shape[1], finish)
+    for copy in (corner_low, corner_high, side_low, top_high, top_low, side_high):
+        copy.wait_send()
+    for copy in first.values():
+        copy.wait_send()
+
+
 def plane_scatter(far, near):
     reps, cores = lax.axis_size("rep"), lax.axis_size("tp")
     rows = near.shape[0] // reps
     far = far.reshape(cores - 1, reps, rows, far.shape[1])
     near = near.reshape(reps, rows, near.shape[1])
+    if in_square(reps, rows):
+        return call_kernel(
+            functools.partial(square_scatter_kernel, cores),
+            2,
+            jax.ShapeDtypeStruct(near.shape[1:], jnp.float32),
+            [
+                pltpu.VMEM(far.shape, jnp.bfloat16),
+                pltpu.VMEM((3, *near.shape[1:]), jnp.bfloat16),
+                pltpu.VMEM((2, *near.shape[1:]), jnp.bfloat16),
+                pltpu.VMEM((2, rows // 2, near.shape[2]), jnp.bfloat16),
+                pltpu.SemaphoreType.DMA((cores, 4)),
+                pltpu.SemaphoreType.DMA((cores, 4)),
+                pltpu.SemaphoreType.DMA((6,)),
+                pltpu.SemaphoreType.DMA((6,)),
+            ],
+            (far, near),
+            28,
+        )
     return call_kernel(
         functools.partial(plane_scatter_kernel, reps, cores),
         2,
@@ -694,11 +884,21 @@
     entry_blocks = own_block(feedforward_entry_matrix)
     down_blocks = own_block(down_weight)
     near_rows = reps * own_rows
+    both_width = joined_width + heads_width
+    full_both = weight_gather(
+        jnp.concatenate(
+            [
+                weight[index]
+                for index in range(LAYERS)
+                for weight in (query_key_value_weight, output_weight)
+            ],
+            axis=1,
+        )
+    )
     for index in range(LAYERS):
-        full_both = weight_gather(
-            jnp.concatenate([query_key_value_weight[index], output_weight[index]], axis=1)
-        )
-        full_qkv, full_out = full_both[:, :joined_width], full_both[:, joined_width:]
+        start = index * both_width
+        full_qkv = full_both[:, start : start + joined_width]
+        full_out = full_both[:, start + joined_width : start + both_width]
         part_entry = gathered(entry_blocks[index].reshape(depth, 2 * block))
         part_down = gathered(down_blocks[index])
         gains = gains_all[index]
@@ -814,9 +1014,10 @@
         mixed_grad = product(out_grad, full_out).astype(jnp.bfloat16)
         mixed_grad, pending = lax.optimization_barrier((mixed_grad, pending))
         if pending is not None:
-            down_pieces[index + 1], gate_pieces[index + 1], up_pieces[index + 1] = [
+            down_pieces[index + 1], gate_pieces[index + 1], up_pieces[index + 1], wide = [
                 replica_blocks(part) for part in pending
             ]
+            qkv_pieces[index + 1] = jnp.concatenate(wide, axis=0).astype(jnp.float32)
         pending = own_parts
         mixed_grad = mixed_grad.reshape(seqs, span, local_groups, group_index, HEAD_SIZE)
         attention_logits = masked_scores(query_rows, keys_all, seen, root)
@@ -863,11 +1064,14 @@
             [left_product(first_normed, joined_grad), left_product(out_grad, mixed_output)], axis=1
         )
         if index:
-            part = scattered(both, ("shard", "rep"))
-            both_sum = jnp.concatenate(replica_blocks(part), axis=0)
+            wide = both.reshape(shards, reps, depth // reps, both_width).swapaxes(0, 1)
+            wide = scattered(wide.reshape(shards * depth, both_width), "rep")
+            pending = (*pending, scattered(wide))
         else:
+            both, *ready = lax.optimization_barrier((both, *pending[:2]))
+            pending = (*ready, pending[2])
             both_sum = gradient_sum(both)
-        qkv_pieces[index] = both_sum.astype(jnp.float32)
+            qkv_pieces[index] = both_sum.astype(jnp.float32)
     down_pieces[0], gate_pieces[0], up_pieces[0] = [replica_blocks(part) for part in pending]
     grad_gate_up = []
     for gates, ups in zip(gate_pieces, up_pieces):
@@ -886,6 +1090,7 @@
     bias_slots = jnp.where(slots, bias[None], 0.0)
     gains_own = jnp.stack(gain_grads)
     small = jnp.concatenate([gains_own.reshape(-1), bias_slots.reshape(-1)])
+    small, _ = lax.optimization_barrier((small, both_sum))
     small = sum_everywhere(small.reshape(-1, LANES), ("rep", "shard", "tp"), 7).reshape(-1)
     gains_total = small[: gains_own.size].reshape(gains_own.shape)
     bias_slots = small[gains_own.size :].reshape(bias_slots.shape)

time: 1560 us -> 1710 us (1.096)
  waiting for transfers between devices: 132 us -> 449 us
  Pallas kernels: 803 us -> 641 us
    reduce_scatter x6 -> x8, waiting for transfers between devices: 0.03 us -> 289 us  [scattered(): return lax.psum_scatter(grad, axes, scatter_dimension=0, tiled=True)]
    pallas_call x25 -> x24, Pallas kernels: 803 us -> 641 us  [call_kernel(): pl.pallas_call(kernel, out_shape=out_shape, in_specs=[pl.BlockSpec(memory...]
    ppermute x21, waiting for transfers between devices: 129 us -> 152 us  [replica_blocks(): blocks.append(lax.ppermute(part, 'rep', peer_pairs(count, step)))]
    unnamed x299 -> x283, local copies, waits for them, and re-layouts: 55.5 us -> 41.9 us
  transfers between devices with their start and end apart: 32 -> 33, of which waited for: 7 -> 19; matrix products, arithmetic and copies ran while one was open for 28% -> 18% of each run, Pallas kernels for 52% -> 33%
where the time goes in v1:
time: 1710 us; the launch traced here: 1700 us
  Pallas kernels  641 us (37%)
  waiting for transfers between devices  449 us (26%)
  matrix products  271 us (16%)
  other arithmetic  159 us (9%)
  local copies, waits for them, and re-layouts  130 us (8%)
  starting transfers between devices  31.4 us (2%)
  between operations  18 us (1%)
    pallas_call x24, Pallas kernels, call_kernel(): pl.pallas_call(kernel, out_shape=out_shape, in_specs=[pl.BlockSpec(memory...  641 us
    reduce_scatter x8, waiting for transfers between devices, scattered(): return lax.psum_scatter(grad, axes, scatter_dimension=0, tiled=True)  289 us
    ppermute x21, waiting for transfers between devices, replica_blocks(): blocks.append(lax.ppermute(part, 'rep', peer_pairs(count, step)))  152 us
    dot_general x10, matrix products, product(): return jnp.dot(left, right, preferred_element_type=jnp.float32)  76.5 us
    dot_general x10, matrix products, left_product(): lax.dot_general(left, right, (((0,), (0,)), ((), ())), preferred_element_...  65.6 us
    dot_general x12, matrix products, right_product(): lax.dot_general(left, right, (((1,), (1,)), ((), ())), preferred_element_...  63.2 us
    unnamed x283, local copies, waits for them, and re-layouts  41.9 us
  transfers between devices with their start and end apart: 33, of which 19 were waited for; matrix products, arithmetic and copies ran while one was open for 18% of the time, Pallas kernels for 33%

profile of v1, /device:TPU:0, one launch (start us, length us, event | category | flops | bytes accessed | tf_op | source)
XLA Modules:
  0.0 1699.9 jit_solution(8220478748889791777)
XLA Ops:
  11.2 13.8 broadcast_select_fusion
  34.9 148.3 %shard_map.161 = bf16[4,4,96,3584]{3,2,1,0:T(8,128)(2,1)S(1)} custom-call(bf16[4,96,3584]{2,1,0:T(8,128)(2,1)S(1)} %pad_maximum_fusion.10.w_ref), custom_call_target="tpu_custom_call" | custom-call | bytes 150000000 | tf_op jit(solution)/shard_map/pallas_call | solution.py:147
  204.3 47.6 %shard_map.162 = bf16[4,768,128]{2,1,0:T(8,128)(2,1)S(1)} custom-call(bf16[768,128]{1,0:T(8,128)(2,1)S(1)} %bitcast.485), custom_call_target="tpu_custom_call" | custom-call | bytes 36000000 | tf_op jit(solution)/shard_map/pallas_call | solution.py:147
  271.3 25.2 %shard_map.164 = bf16[2,4,192,1536]{3,2,1,0:T(8,128)(2,1)S(1)} custom-call(bf16[192,1536]{1,0:T(8,128)(2,1)S(1)} %multiply_convert_fusion.9.x_ref), custom_call_target="tpu_custom_call" | custom-call | bytes 90000000 | tf_op jit(solution)/shard_map/pallas_call | solution.py:147
  299.1 25.1 %shard_map.172 = bf16[2,4,192,1536]{3,2,1,0:T(8,128)(2,1)S(1)} custom-call(bf16[192,1536]{1,0:T(8,128)(2,1)S(1)} %fusion.127.x_ref), custom_call_target="tpu_custom_call" | custom-call | bytes 90000000 | tf_op jit(solution)/shard_map/pallas_call | solution.py:147
  326.4 11.1 fusion.22
  337.5 9.2 fusion.20
  349.5 11.1 multiply_convert_fusion.5
  370.6 24.8 %shard_map.165 = f32[192,1536]{1,0:T(8,128)S(1)} custom-call(bf16[1,4,192,1536]{3,2,1,0:T(8,128)(2,1)S(1)} %bitcast.476, f32[4,192,1536]{2,1,0:T(8,128)S(1)} %bitcast.468), custom_call_target="tpu_custom_call" | custom-call | bytes 84000000 | tf_op jit(solution)/shard_map/pallas_call | solution.py:147
  404.6 41.6 %shard_map.167 = bf16[4,768,128]{2,1,0:T(8,128)(2,1)S(1)} custom-call(bf16[768,128]{1,0:T(8,128)(2,1)S(1)} %bitcast.486), custom_call_target="tpu_custom_call" | custom-call | bytes 36000000 | tf_op jit(solution)/shard_map/pallas_call | solution.py:147
  463.5 25.0 %shard_map.169 = bf16[2,4,192,1536]{3,2,1,0:T(8,128)(2,1)S(1)} custom-call(bf16[192,1536]{1,0:T(8,128)(2,1)S(1)} %multiply_convert_fusion.7.x_ref), custom_call_target="tpu_custom_call" | custom-call | bytes 90000000 | tf_op jit(solution)/shard_map/pallas_call | solution.py:147
  495.4 9.4 fusion.16
  504.8 13.6 multiply_convert_fusion.4
  518.4 9.9 convolution_convert_fusion.5
  536.4 10.7 multiply_convert_fusion.3
  556.5 10.5 convolution_convert_fusion.4
  573.7 9.2 fusion.38
  589.1 25.3 %shard_map.173 = f32[192,1536]{1,0:T(8,128)S(1)} custom-call(bf16[1,4,192,1536]{3,2,1,0:T(8,128)(2,1)S(1)} %bitcast.473, f32[4,192,1536]{2,1,0:T(8,128)S(1)} %bitcast.465), custom_call_target="tpu_custom_call" | custom-call | bytes 84000000 | tf_op jit(solution)/shard_map/pallas_call | solution.py:147
  622.1 24.5 %shard_map.170 = f32[192,1536]{1,0:T(8,128)S(1)} custom-call(bf16[1,4,192,1536]{3,2,1,0:T(8,128)(2,1)S(1)} %bitcast.474, f32[4,192,1536]{2,1,0:T(8,128)S(1)} %bitcast.466), custom_call_target="tpu_custom_call" | custom-call | bytes 84000000 | tf_op jit(solution)/shard_map/pallas_call | solution.py:147
  655.4 12.8 fusion.3
  696.9 25.4 %shard_map.175 = f32[768,128]{1,0:T(8,128)S(1)} custom-call(bf16[3,768,128]{2,1,0:T(8,128)(2,1)S(1)} %bitcast.471, f32[768,128]{1,0:T(8,128)S(1)} %bitcast.477), custom_call_target="tpu_custom_call" | custom-call | bytes 42000000 | tf_op jit(solution)/shard_map/pallas_call | solution.py:147
  758.2 44.0 %shard_map.177 = bf16[2,4,192,1536]{3,2,1,0:T(8,128)(2,1)S(1)} custom-call(bf16[192,1536]{1,0:T(8,128)(2,1)S(1)} %get-tuple-element.62.x_ref), custom_call_target="tpu_custom_call" | custom-call | bytes 90000000 | tf_op jit(solution)/shard_map/pallas_call | solution.py:147
  812.1 10.9 fusion.28
  831.1 11.7 multiply_convert_fusion.1
  849.3 10.0 convolution_convert_fusion
  859.3 10.4 convolution_convert_fusion.1
  873.5 9.4 fusion.34
  892.0 24.5 %shard_map.178 = f32[192,1536]{1,0:T(8,128)S(1)} custom-call(bf16[1,4,192,1536]{3,2,1,0:T(8,128)(2,1)S(1)} %bitcast.475, f32[4,192,1536]{2,1,0:T(8,128)S(1)} %bitcast.467), custom_call_target="tpu_custom_call" | custom-call | bytes 84000000 | tf_op jit(solution)/shard_map/pallas_call | solution.py:147
  924.9 14.6 reduce-scatter.23.cloned.1.call-done
  948.6 13.6 collective-permute-done.6
  962.2 18.6 %collective-permute-done.7 = bf16[384,1152]{1,0:T(8,128)(2,1)S(1)} collective-permute-done((bf16[384,1152]{1,0:T(8,128)(2,1)}, bf16[384,1152]{1,0:T(8,128)(2,1)S(1)}, u32[]{:S(2)}, u32[]{:S(2)}) %collective-permute-start.7) | collective-permute-done | bytes 884768 | tf_op jit(solution)/shard_map/ppermute | solution.py:778
  983.1 25.4 %reduce-scatter.11.cloned.1.call-done = bf16[384,1152]{1,0:T(8,128)(2,1)} async-done(((bf16[1536,1152]{1,0:T(8,128)(2,1)}), bf16[384,1152]{1,0:T(8,128)(2,1)}) %reduce-scatter.11.cloned.1.call-update) | async-done | bytes 884752 | tf_op jit(solution)/shard_map/reduce_scatter | solution.py:802
  1008.5 69.0 %reduce-scatter.13.cloned.1.call-done = bf16[384,1152]{1,0:T(8,128)(2,1)} async-done(((bf16[1536,1152]{1,0:T(8,128)(2,1)}), bf16[384,1152]{1,0:T(8,128)(2,1)}) %reduce-scatter.13.cloned.1.call-update) | async-done | bytes 884752 | tf_op jit(solution)/shard_map/reduce_scatter | solution.py:802
  1077.5 69.0 %reduce-scatter.9.cloned.1.call-done = bf16[384,1152]{1,0:T(8,128)(2,1)} async-done(((bf16[1536,1152]{1,0:T(8,128)(2,1)}), bf16[384,1152]{1,0:T(8,128)(2,1)}) %reduce-scatter.9.cloned.1.call-update) | async-done | bytes 884752 | tf_op jit(solution)/shard_map/reduce_scatter | solution.py:802
  1146.5 34.7 %reduce-scatter.17.cloned.1.call-done = bf16[96,1792]{1,0:T(8,128)(2,1)} async-done(((bf16[384,1792]{1,0:T(8,128)(2,1)}), bf16[96,1792]{1,0:T(8,128)(2,1)}) %reduce-scatter.17.cloned.1.call-update) | async-done | bytes 344080 | tf_op jit(solution)/shard_map/reduce_scatter | solution.py:802
  1181.6 13.3 fusion
  1218.6 26.6 %shard_map.180 = f32[768,128]{1,0:T(8,128)S(1)} custom-call(bf16[3,768,128]{2,1,0:T(8,128)(2,1)S(1)} %bitcast.472, f32[768,128]{1,0:T(8,128)S(1)} %bitcast.478), custom_call_target="tpu_custom_call" | custom-call | bytes 42000000 | tf_op jit(solution)/shard_map/pallas_call | solution.py:147
  1261.4 71.8 %reduce-scatter.19.cloned.1.call-done = bf16[384,1152]{1,0:T(8,128)(2,1)} async-done(((bf16[1536,1152]{1,0:T(8,128)(2,1)}), bf16[384,1152]{1,0:T(8,128)(2,1)}) %reduce-scatter.19.cloned.1.call-update) | async-done | bytes 884752 | tf_op jit(solution)/shard_map/reduce_scatter | solution.py:802
  1345.9 32.9 %shard_map.184 = f32[80,128]{1,0:T(8,128)S(1)} custom-call(f32[80,128]{1,0:T(8,128)S(1)} %bitcast.487), custom_call_target="tpu_custom_call" | custom-call | bytes 24000000 | tf_op jit(solution)/shard_map/pallas_call | solution.py:147
  1392.3 80.3 %shard_map.183 = bf16[4,96,1792]{2,1,0:T(8,128)(2,1)S(1)} custom-call(bf16[4,4,96,1792]{3,2,1,0:T(8,128)(2,1)S(1)} %bitcast.432), custom_call_target="tpu_custom_call" | custom-call | bytes 270000000 | tf_op jit(solution)/shard_map/pallas_call | solution.py:147
  1487.7 13.3 collective-permute-done.3
  1502.8 35.3 %collective-permute-done.4 = bf16[384,1152]{1,0:T(8,128)(2,1)S(1)} collective-permute-done((bf16[384,1152]{1,0:T(8,128)(2,1)S(1)}, bf16[384,1152]{1,0:T(8,128)(2,1)S(1)}, u32[]{:S(2)}, u32[]{:S(2)}) %collective-permute-start.4) | collective-permute-done | bytes 884768 | tf_op jit(solution)/shard_map/ppermute | solution.py:778
  1563.3 17.0 %collective-permute-done.19 = bf16[384,1152]{1,0:T(8,128)(2,1)S(1)} collective-permute-done((bf16[384,1152]{1,0:T(8,128)(2,1)S(1)}, bf16[384,1152]{1,0:T(8,128)(2,1)S(1)}, u32[]{:S(2)}, u32[]{:S(2)}) %collective-permute-start.19) | collective-permute-done | bytes 884768 | tf_op jit(solution)/shard_map/ppermute | solution.py:778
  1601.3 17.0 %collective-permute-done.10 = bf16[384,1152]{1,0:T(8,128)(2,1)} collective-permute-done((bf16[384,1152]{1,0:T(8,128)(2,1)}, bf16[384,1152]{1,0:T(8,128)(2,1)}, u32[]{:S(2)}, u32[]{:S(2)}) %collective-permute-start.10) | collective-permute-done | bytes 884768 | tf_op jit(solution)/shard_map/ppermute | solution.py:778
  1623.7 13.0 collective-permute-done.12
  1636.6 15.0 collective-permute-done.13
  1669.7 9.3 maximum_convert_fusion.1
  1679.1 13.5 maximum_convert_fusion
  (574 shorter events, 423.5 us)
Async XLA Ops:
  7.2 319.2 %all-gather.13.cloned.1.call-start = ((), (), s32[]{:S(2)}) async-start(), calls=%async_computation.19 | async-start | bytes 4423680 | tf_op jit(solution)/shard_map/all_gather | solution.py:798
  11.2 326.3 %all-gather.7.cloned.1.call-start = ((), (), s32[]{:S(2)}) async-start(), calls=%async_computation.8 | async-start | bytes 8847360 | tf_op jit(solution)/shard_map/all_gather | solution.py:798
  29.2 331.4 %all-gather.11.cloned.1.call-start = ((), (), s32[]{:S(2)}) async-start(), calls=%async_computation.18 | async-start | bytes 4423680 | tf_op jit(solution)/shard_map/all_gather | solution.py:798
  30.0 465.4 %all-gather.9.cloned.1.call-start = ((), (), s32[]{:S(2)}) async-start(), calls=%async_computation.9 | async-start | bytes 8847360 | tf_op jit(solution)/shard_map/all_gather | solution.py:798
  31.5 840.6 %reduce-scatter.15.cloned.1.call-start = ((), (), s32[]{:S(2)}) async-start(), calls=%async_computation.13 | async-start | bytes 6881280 | tf_op jit(solution)/shard_map/reduce_scatter | solution.py:802
  34.1 150.9 %copy-start.44 = (bf16[1,384,1536]{2,1,0:T(8,128)(2,1)}, bf16[1,384,1536]{2,1,0:T(8,128)(2,1)S(1)}, u32[]{:S(2)}) copy-start(bf16[1,384,1536]{2,1,0:T(8,128)(2,1)S(1)} %get-tuple-element.73) | copy-start | bytes 3538948
  34.4 150.6 %copy-start.112 = (f32[384]{0:T(512)}, f32[384]{0:T(512)S(1)}, u32[]{:S(2)}) copy-start(f32[384]{0:T(512)S(1)} %add_rsqrt_fusion) | copy-start | bytes 4612
  34.9 148.3 %copy-start.106 = (bf16[2,2,1536]{2,1,0:T(2,128)(2,1)S(1)}, bf16[2,2,1536]{2,1,0:T(2,128)(2,1)}, u32[]{:S(2)}) copy-start(bf16[2,2,1536]{2,1,0:T(2,128)(2,1)} %param.16) | copy-start | bytes 36868
  34.9 149.1 %copy-start.101 = (bf16[2,1024]{1,0:T(2,128)(2,1)S(1)}, bf16[2,1024]{1,0:T(2,128)(2,1)}, u32[]{:S(2)}) copy-start(bf16[2,1024]{1,0:T(2,128)(2,1)} %param.12) | copy-start | bytes 12292
  183.9 87.2 %copy-start.86 = (f32[1536]{0:T(1024)}, f32[1536]{0:T(1024)S(1)}, u32[]{:S(2)}) copy-start(f32[1536]{0:T(1024)S(1)} %get-tuple-element.54) | copy-start | bytes 18436
  183.9 212.3 %copy-start.88 = (f32[1536]{0:T(1024)}, f32[1536]{0:T(1024)S(1)}, u32[]{:S(2)}) copy-start(f32[1536]{0:T(1024)S(1)} %get-tuple-element.53) | copy-start | bytes 18436
  191.0 61.0 %copy-start.69 = (f32[1,1,384,1,64]{4,2,3,1,0:T(8,128)}, f32[1,1,384,1,64]{4,2,3,1,0:T(8,128)S(1)}, u32[]{:S(2)}) copy-start(f32[1,1,384,1,64]{4,2,3,1,0:T(8,128)S(1)} %get-tuple-element.156) | copy-start | bytes 294916
  202.5 49.5 %copy-start.107 = (pred[1536]{0:T(1024)(128)(4,1)S(1)}, pred[1536]{0:T(1024)(128)(4,1)}, u32[]{:S(2)}) copy-start(pred[1536]{0:T(1024)(128)(4,1)} %broadcast_compare_fusion) | copy-start | bytes 4612
  202.6 51.5 %copy-start.65 = (f32[384,128]{0,1:T(8,128)S(1)}, f32[384,128]{0,1:T(8,128)}, u32[]{:S(2)}) copy-start(f32[384,128]{0,1:T(8,128)} %copy.147) | copy-start | bytes 589828
  202.6 51.5 %copy-start.67 = (f32[384,128]{0,1:T(8,128)S(1)}, f32[384,128]{0,1:T(8,128)}, u32[]{:S(2)}) copy-start(f32[384,128]{0,1:T(8,128)} %copy.148) | copy-start | bytes 589828
  270.4 124.9 %copy-start.14 = (f32[192,1536]{1,0:T(8,128)}, f32[192,1536]{1,0:T(8,128)S(1)}, u32[]{:S(2)}) copy-start(f32[192,1536]{1,0:T(8,128)S(1)} %get-tuple-element.71) | copy-start | bytes 3538948
  751.4 188.1 %reduce-scatter.23.cloned.1.call-start = ((), (), s32[]{:S(2)}) async-start(), calls=%async_computation.17 | async-start | bytes 4423680 | tf_op jit(solution)/shard_map/reduce_scatter | solution.py:802
  869.8 138.7 %reduce-scatter.11.cloned.1.call-start = ((), (), s32[]{:S(2)}) async-start(), calls=%async_computation.11 | async-start | bytes 4423680 | tf_op jit(solution)/shard_map/reduce_scatter | solution.py:802
  870.5 207.0 %reduce-scatter.13.cloned.1.call-start = ((), (), s32[]{:S(2)}) async-start(), calls=%async_computation.12 | async-start | bytes 4423680 | tf_op jit(solution)/shard_map/reduce_scatter | solution.py:802
  871.3 275.2 %reduce-scatter.9.cloned.1.call-start = ((), (), s32[]{:S(2)}) async-start(), calls=%async_computation.10 | async-start | bytes 4423680 | tf_op jit(solution)/shard_map/reduce_scatter | solution.py:802
  872.0 309.2 %reduce-scatter.17.cloned.1.call-start = ((), (), s32[]{:S(2)}) async-start(), calls=%async_computation.14 | async-start | bytes 1720320 | tf_op jit(solution)/shard_map/reduce_scatter | solution.py:802
  872.6 388.8 %reduce-scatter.21.cloned.1.call-start = ((), (), s32[]{:S(2)}) async-start(), calls=%async_computation.16 | async-start | bytes 4423680 | tf_op jit(solution)/shard_map/reduce_scatter | solution.py:802
  873.4 459.8 %reduce-scatter.19.cloned.1.call-start = ((), (), s32[]{:S(2)}) async-start(), calls=%async_computation.15 | async-start | bytes 4423680 | tf_op jit(solution)/shard_map/reduce_scatter | solution.py:802
  939.5 22.7 %collective-permute-start.6 = (bf16[384,1152]{1,0:T(8,128)(2,1)}, bf16[384,1152]{1,0:T(8,128)(2,1)S(1)}, u32[]{:S(2)}, u32[]{:S(2)}) collective-permute-start(bf16[384,1152]{1,0:T(8,128)(2,1)} %reduce-scatter.23.cloned.1.call-done), channel_id=1, source_target_pairs={{0,8},{8,0},{16,24},{24,16},{1,9},{9,1},{17,25},{25,17},{2,10},{10... | collective-permute-start | bytes 2654216 | tf_op jit(solution)/shard_map/ppermute | solution.py:778
  940.9 39.9 %collective-permute-start.7 = (bf16[384,1152]{1,0:T(8,128)(2,1)}, bf16[384,1152]{1,0:T(8,128)(2,1)S(1)}, u32[]{:S(2)}, u32[]{:S(2)}) collective-permute-start(bf16[384,1152]{1,0:T(8,128)(2,1)} %reduce-scatter.23.cloned.1.call-done), channel_id=1, source_target_pairs={{0,16},{8,24},{16,0},{24,8},{1,17},{9,25},{17,1},{25,9},{2,18},{10... | collective-permute-start | bytes 2654216 | tf_op jit(solution)/shard_map/ppermute | solution.py:778
  942.4 38.4 %collective-permute-start.8 = (bf16[384,1152]{1,0:T(8,128)(2,1)}, bf16[384,1152]{1,0:T(8,128)(2,1)S(1)}, u32[]{:S(2)}, u32[]{:S(2)}) collective-permute-start(bf16[384,1152]{1,0:T(8,128)(2,1)} %reduce-scatter.23.cloned.1.call-done), channel_id=1, source_target_pairs={{0,24},{8,16},{16,8},{24,0},{1,25},{9,17},{17,9},{25,1},{2,26},{10... | collective-permute-start | bytes 2654216 | tf_op jit(solution)/shard_map/ppermute | solution.py:778
  981.4 200.2 %copy-start.48 = (bf16[1,1,4,384,1,128]{5,3,0,2,4,1:T(8,128)(2,1)S(1)}, bf16[1,1,4,384,1,128]{5,3,0,2,4,1:T(8,128)(2,1)}, u32[]{:S(2)}) copy-start(bf16[1,1,4,384,1,128]{5,3,0,2,4,1:T(8,128)(2,1)} %copy-done.47) | copy-start | bytes 1179652
  981.4 200.2 %copy-start.85 = (f32[6,384]{1,0:T(8,128)S(1)}, f32[6,384]{1,0:T(8,128)}, u32[]{:S(2)}) copy-start(f32[6,384]{1,0:T(8,128)} %copy-done.84) | copy-start | bytes 27652
  1333.2 210.5 %collective-permute-start.15 = (bf16[384,1152]{1,0:T(8,128)(2,1)}, bf16[384,1152]{1,0:T(8,128)(2,1)}, u32[]{:S(2)}, u32[]{:S(2)}) collective-permute-start(bf16[384,1152]{1,0:T(8,128)(2,1)} %reduce-scatter.19.cloned.1.call-done), channel_id=1, source_target_pairs={{0,8},{8,0},{16,24},{24,16},{1,9},{9,1},{17,25},{25,17},{2,10},{10... | collective-permute-start | bytes 2654216 | tf_op jit(solution)/shard_map/ppermute | solution.py:778
  1334.6 210.0 %collective-permute-start.16 = (bf16[384,1152]{1,0:T(8,128)(2,1)}, bf16[384,1152]{1,0:T(8,128)(2,1)}, u32[]{:S(2)}, u32[]{:S(2)}) collective-permute-start(bf16[384,1152]{1,0:T(8,128)(2,1)} %reduce-scatter.19.cloned.1.call-done), channel_id=1, source_target_pairs={{0,16},{8,24},{16,0},{24,8},{1,17},{9,25},{17,1},{25,9},{2,18},{10... | collective-permute-start | bytes 2654216 | tf_op jit(solution)/shard_map/ppermute | solution.py:778
  1336.1 142.3 %collective-permute-start = (bf16[96,1792]{1,0:T(8,128)(2,1)}, bf16[96,1792]{1,0:T(8,128)(2,1)}, u32[]{:S(2)}, u32[]{:S(2)}) collective-permute-start(bf16[96,1792]{1,0:T(8,128)(2,1)} %reduce-scatter.17.cloned.1.call-done), channel_id=1, source_target_pairs={{0,8},{8,0},{16,24},{24,16},{1,9},{9,1},{17,25},{25,17},{2,10},{10... | collective-permute-start | bytes 1032200 | tf_op jit(solution)/shard_map/ppermute | solution.py:778
  1336.7 142.3 %collective-permute-start.1 = (bf16[96,1792]{1,0:T(8,128)(2,1)}, bf16[96,1792]{1,0:T(8,128)(2,1)}, u32[]{:S(2)}, u32[]{:S(2)}) collective-permute-start(bf16[96,1792]{1,0:T(8,128)(2,1)} %reduce-scatter.17.cloned.1.call-done), channel_id=1, source_target_pairs={{0,16},{8,24},{16,0},{24,8},{1,17},{9,25},{17,1},{25,9},{2,18},{10... | collective-permute-start | bytes 1032200 | tf_op jit(solution)/shard_map/ppermute | solution.py:778
  1337.2 143.6 %collective-permute-start.2 = (bf16[96,1792]{1,0:T(8,128)(2,1)}, bf16[96,1792]{1,0:T(8,128)(2,1)}, u32[]{:S(2)}, u32[]{:S(2)}) collective-permute-start(bf16[96,1792]{1,0:T(8,128)(2,1)} %reduce-scatter.17.cloned.1.call-done), channel_id=1, source_target_pairs={{0,24},{8,16},{16,8},{24,0},{1,25},{9,17},{17,9},{25,1},{2,26},{10... | collective-permute-start | bytes 1032200 | tf_op jit(solution)/shard_map/ppermute | solution.py:778
  1392.3 80.3 %slice-start.8 = ((f32[80,128]{1,0:T(8,128)}), f32[48,128]{1,0:T(8,128)S(1)}, s32[]{:S(2)}) async-start(f32[80,128]{1,0:T(8,128)} %copy-done.9), calls=%async_computation.28 | async-start | bytes 49152 | tf_op jit(solution)/shard_map/slice | solution.py:1095
  1478.4 22.5 %collective-permute-start.3 = (bf16[384,1152]{1,0:T(8,128)(2,1)S(1)}, bf16[384,1152]{1,0:T(8,128)(2,1)S(1)}, u32[]{:S(2)}, u32[]{:S(2)}) collective-permute-start(bf16[384,1152]{1,0:T(8,128)(2,1)S(1)} %copy-done.77), channel_id=1, source_target_pairs={{0,8},{8,0},{16,24},{24,16},{1,9},{9,1},{17,25},{25,17},{2,10},{10... | collective-permute-start | bytes 2654216 | tf_op jit(solution)/shard_map/ppermute | solution.py:778
  1479.0 59.1 %collective-permute-start.4 = (bf16[384,1152]{1,0:T(8,128)(2,1)S(1)}, bf16[384,1152]{1,0:T(8,128)(2,1)S(1)}, u32[]{:S(2)}, u32[]{:S(2)}) collective-permute-start(bf16[384,1152]{1,0:T(8,128)(2,1)S(1)} %copy-done.77), channel_id=1, source_target_pairs={{0,16},{8,24},{16,0},{24,8},{1,17},{9,25},{17,1},{25,9},{2,18},{10... | collective-permute-start | bytes 2654216 | tf_op jit(solution)/shard_map/ppermute | solution.py:778
  1480.8 57.9 %collective-permute-start.5 = (bf16[384,1152]{1,0:T(8,128)(2,1)S(1)}, bf16[384,1152]{1,0:T(8,128)(2,1)S(1)}, u32[]{:S(2)}, u32[]{:S(2)}) collective-permute-start(bf16[384,1152]{1,0:T(8,128)(2,1)S(1)} %copy-done.77), channel_id=1, source_target_pairs={{0,24},{8,16},{16,8},{24,0},{1,25},{9,17},{17,9},{25,1},{2,26},{10... | collective-permute-start | bytes 2654216 | tf_op jit(solution)/shard_map/ppermute | solution.py:778
  1486.1 52.0 %copy-start.76 = (bf16[384,1152]{1,0:T(8,128)(2,1)S(1)}, bf16[384,1152]{1,0:T(8,128)(2,1)}, u32[]{:S(2)}) copy-start(bf16[384,1152]{1,0:T(8,128)(2,1)} %reduce-scatter.9.cloned.1.call-done) | copy-start | bytes 2654212
  1501.0 44.3 %collective-permute-start.17 = (bf16[384,1152]{1,0:T(8,128)(2,1)S(1)}, bf16[384,1152]{1,0:T(8,128)(2,1)S(1)}, u32[]{:S(2)}, u32[]{:S(2)}) collective-permute-start(bf16[384,1152]{1,0:T(8,128)(2,1)S(1)} %copy-done.78), channel_id=1, source_target_pairs={{0,24},{8,16},{16,8},{24,0},{1,25},{9,17},{17,9},{25,1},{2,26},{10... | collective-permute-start | bytes 2654216 | tf_op jit(solution)/shard_map/ppermute | solution.py:778
  1538.1 22.5 %collective-permute-start.18 = (bf16[384,1152]{1,0:T(8,128)(2,1)S(1)}, bf16[384,1152]{1,0:T(8,128)(2,1)S(1)}, u32[]{:S(2)}, u32[]{:S(2)}) collective-permute-start(bf16[384,1152]{1,0:T(8,128)(2,1)S(1)} %copy-done.76), channel_id=1, source_target_pairs={{0,8},{8,0},{16,24},{24,16},{1,9},{9,1},{17,25},{25,17},{2,10},{10... | collective-permute-start | bytes 2654216 | tf_op jit(solution)/shard_map/ppermute | solution.py:778
  1538.7 41.6 %collective-permute-start.19 = (bf16[384,1152]{1,0:T(8,128)(2,1)S(1)}, bf16[384,1152]{1,0:T(8,128)(2,1)S(1)}, u32[]{:S(2)}, u32[]{:S(2)}) collective-permute-start(bf16[384,1152]{1,0:T(8,128)(2,1)S(1)} %copy-done.76), channel_id=1, source_target_pairs={{0,16},{8,24},{16,0},{24,8},{1,17},{9,25},{17,1},{25,9},{2,18},{10... | collective-permute-start | bytes 2654216 | tf_op jit(solution)/shard_map/ppermute | solution.py:778
  1543.7 38.4 %collective-permute-start.20 = (bf16[384,1152]{1,0:T(8,128)(2,1)S(1)}, bf16[384,1152]{1,0:T(8,128)(2,1)S(1)}, u32[]{:S(2)}, u32[]{:S(2)}) collective-permute-start(bf16[384,1152]{1,0:T(8,128)(2,1)S(1)} %copy-done.76), channel_id=1, source_target_pairs={{0,24},{8,16},{16,8},{24,0},{1,25},{9,17},{17,9},{25,1},{2,26},{10... | collective-permute-start | bytes 2654216 | tf_op jit(solution)/shard_map/ppermute | solution.py:778
  1544.6 54.6 %collective-permute-start.9 = (bf16[384,1152]{1,0:T(8,128)(2,1)}, bf16[384,1152]{1,0:T(8,128)(2,1)}, u32[]{:S(2)}, u32[]{:S(2)}) collective-permute-start(bf16[384,1152]{1,0:T(8,128)(2,1)} %reduce-scatter.11.cloned.1.call-done), channel_id=1, source_target_pairs={{0,8},{8,0},{16,24},{24,16},{1,9},{9,1},{17,25},{25,17},{2,10},{10... | collective-permute-start | bytes 2654216 | tf_op jit(solution)/shard_map/ppermute | solution.py:778
  1545.3 73.1 %collective-permute-start.10 = (bf16[384,1152]{1,0:T(8,128)(2,1)}, bf16[384,1152]{1,0:T(8,128)(2,1)}, u32[]{:S(2)}, u32[]{:S(2)}) collective-permute-start(bf16[384,1152]{1,0:T(8,128)(2,1)} %reduce-scatter.11.cloned.1.call-done), channel_id=1, source_target_pairs={{0,16},{8,24},{16,0},{24,8},{1,17},{9,25},{17,1},{25,9},{2,18},{10... | collective-permute-start | bytes 2654216 | tf_op jit(solution)/shard_map/ppermute | solution.py:778
  1560.6 59.2 %collective-permute-start.11 = (bf16[384,1152]{1,0:T(8,128)(2,1)}, bf16[384,1152]{1,0:T(8,128)(2,1)}, u32[]{:S(2)}, u32[]{:S(2)}) collective-permute-start(bf16[384,1152]{1,0:T(8,128)(2,1)} %reduce-scatter.11.cloned.1.call-done), channel_id=1, source_target_pairs={{0,24},{8,16},{16,8},{24,0},{1,25},{9,17},{17,9},{25,1},{2,26},{10... | collective-permute-start | bytes 2654216 | tf_op jit(solution)/shard_map/ppermute | solution.py:778
  1580.3 56.3 %collective-permute-start.12 = (bf16[384,1152]{1,0:T(8,128)(2,1)}, bf16[384,1152]{1,0:T(8,128)(2,1)}, u32[]{:S(2)}, u32[]{:S(2)}) collective-permute-start(bf16[384,1152]{1,0:T(8,128)(2,1)} %reduce-scatter.13.cloned.1.call-done), channel_id=1, source_target_pairs={{0,8},{8,0},{16,24},{24,16},{1,9},{9,1},{17,25},{25,17},{2,10},{10... | collective-permute-start | bytes 2654216 | tf_op jit(solution)/shard_map/ppermute | solution.py:778
  1582.1 69.5 %collective-permute-start.13 = (bf16[384,1152]{1,0:T(8,128)(2,1)}, bf16[384,1152]{1,0:T(8,128)(2,1)}, u32[]{:S(2)}, u32[]{:S(2)}) collective-permute-start(bf16[384,1152]{1,0:T(8,128)(2,1)} %reduce-scatter.13.cloned.1.call-done), channel_id=1, source_target_pairs={{0,16},{8,24},{16,0},{24,8},{1,17},{9,25},{17,1},{25,9},{2,18},{10... | collective-permute-start | bytes 2654216 | tf_op jit(solution)/shard_map/ppermute | solution.py:778
  1599.2 53.1 %collective-permute-start.14 = (bf16[384,1152]{1,0:T(8,128)(2,1)}, bf16[384,1152]{1,0:T(8,128)(2,1)S(1)}, u32[]{:S(2)}, u32[]{:S(2)}) collective-permute-start(bf16[384,1152]{1,0:T(8,128)(2,1)} %reduce-scatter.13.cloned.1.call-done), channel_id=1, source_target_pairs={{0,24},{8,16},{16,8},{24,0},{1,25},{9,17},{17,9},{25,1},{2,26},{10... | collective-permute-start | bytes 2654216 | tf_op jit(solution)/shard_map/ppermute | solution.py:778
  (124 other events, 1443.5 us)
Sparse Core Ops, SparseCore 0:
  11.3 122.6 all-gather.12
  136.2 143.3 all-gather.6
  281.8 68.0 all-gather.10
  351.9 143.4 all-gather.8
  751.5 84.8 reduce-scatter.14
  869.9 69.5 reduce-scatter.22
  941.8 66.6 reduce-scatter.10
  1010.8 66.6 reduce-scatter.12
  1079.8 66.6 reduce-scatter.8
  1148.7 32.5 reduce-scatter.16
  1183.6 77.7 reduce-scatter.20
  1263.6 69.5 reduce-scatter.18

commit v2 on v1

--- a/solution.py
+++ b/solution.py
@@ -770,12 +770,16 @@
     return [((i + step) % count, i) for i in range(count)]
 
 
-def replica_blocks(part):
+def from_replicas(part):
+    count = lax.axis_size("rep")
+    return [part] + [
+        lax.ppermute(part, "rep", peer_pairs(count, step)) for step in range(1, count)
+    ]
+
+
+def in_order(blocks):
     count = lax.axis_size("rep")
     me = lax.axis_index("rep")
-    blocks = [part]
-    for step in range(1, count):
-        blocks.append(lax.ppermute(part, "rep", peer_pairs(count, step)))
     held = jnp.stack(blocks)
     places = []
     for index in range(count):
@@ -899,8 +903,14 @@
         start = index * both_width
         full_qkv = full_both[:, start : start + joined_width]
         full_out = full_both[:, start + joined_width : start + both_width]
-        part_entry = gathered(entry_blocks[index].reshape(depth, 2 * block))
-        part_down = gathered(down_blocks[index])
+        entry_block = entry_blocks[index].reshape(depth, 2 * block)
+        if index:
+            part = jnp.concatenate([entry_block, down_blocks[index]], axis=1)
+            part = gathered(part)
+            part_entry, part_down = part[:, : 2 * block], part[:, 2 * block :]
+        else:
+            part_entry = gathered(entry_block)
+            part_down = gathered(down_blocks[index])
         gains = gains_all[index]
         scale_one = norm_scale(residual_state)
         if index:
@@ -991,9 +1001,12 @@
         ) = saved[index]
         gains = gains_all[index]
         plane_grad = plane_gather(flow.astype(jnp.bfloat16))
+        down_total = left_product(plane_grad, hidden_state)
+        plane_grad, down_total = lax.optimization_barrier((plane_grad, down_total))
+        if pending is not None:
+            plane_grad, part = lax.optimization_barrier((plane_grad, pending[0]))
+            gate_pieces[index + 1] = from_replicas(part)
         hidden_grad = product(plane_grad, part_down)
-        down_total = left_product(plane_grad, hidden_state)
-        hidden_grad, down_total = lax.optimization_barrier((hidden_grad, down_total))
         down_own = scattered(down_total)
         sigmoid = jax.nn.sigmoid(gate)
         gate_grad = hidden_grad * upper * (sigmoid + gate * sigmoid * (1.0 - sigmoid))
@@ -1004,7 +1017,10 @@
         entry_grad, gate_total, up_total = lax.optimization_barrier(
             (entry_grad, gate_total, up_total)
         )
-        own_parts = (down_own, scattered(gate_total), scattered(up_total))
+        if pending is not None:
+            entry_grad, part = lax.optimization_barrier((entry_grad, pending[1]))
+            up_pieces[index + 1] = from_replicas(part)
+        own_parts = (scattered(gate_total), scattered(up_total))
         far_product = right_product(entry_grad[near_rows:], part_entry).astype(jnp.bfloat16)
         near_product = right_product(entry_grad[:near_rows], part_entry)
         normed_two_grad = plane_scatter(far_product, near_product)
@@ -1012,12 +1028,9 @@
         middle_grad = flow + middle_grad
         out_grad = core_gather(middle_grad.astype(jnp.bfloat16), 3)
         mixed_grad = product(out_grad, full_out).astype(jnp.bfloat16)
-        mixed_grad, pending = lax.optimization_barrier((mixed_grad, pending))
         if pending is not None:
-            down_pieces[index + 1], gate_pieces[index + 1], up_pieces[index + 1], wide = [
-                replica_blocks(part) for part in pending
-            ]
-            qkv_pieces[index + 1] = jnp.concatenate(wide, axis=0).astype(jnp.float32)
+            mixed_grad, wide = lax.optimization_barrier((mixed_grad, pending[2]))
+            qkv_pieces[index + 1] = from_replicas(wide)
         pending = own_parts
         mixed_grad = mixed_grad.reshape(seqs, span, local_groups, group_index, HEAD_SIZE)
         attention_logits = masked_scores(query_rows, keys_all, seen, root)
@@ -1047,6 +1060,8 @@
         pair = pair.reshape(2, seqs, shards, span, local_groups, HEAD_SIZE)
         pair = jnp.moveaxis(pair, 2, 0).reshape(shards, -1, HEAD_SIZE)
         pair_own = ring_scatter(pair[1:].astype(jnp.bfloat16), pair[0], "shard", 6, 14)
+        pair_own, down_own = lax.optimization_barrier((pair_own, down_own))
+        down_pieces[index] = from_replicas(down_own)
         pair_own = pair_own.reshape(2, seqs, span, local_groups, HEAD_SIZE)
         key_own, value_own = pair_own[0], pair_own[1]
         unrotated_asks = rotate_back(query_grad, cos_query, sin_query)
@@ -1068,11 +1083,19 @@
             wide = scattered(wide.reshape(shards * depth, both_width), "rep")
             pending = (*pending, scattered(wide))
         else:
-            both, *ready = lax.optimization_barrier((both, *pending[:2]))
-            pending = (*ready, pending[2])
-            both_sum = gradient_sum(both)
-            qkv_pieces[index] = both_sum.astype(jnp.float32)
-    down_pieces[0], gate_pieces[0], up_pieces[0] = [replica_blocks(part) for part in pending]
+            both_sum, *pending = lax.optimization_barrier((gradient_sum(both), *pending))
+    both_sum, *late = lax.optimization_barrier(
+        (both_sum, gate_pieces[1:], up_pieces[1:], down_pieces[1:], qkv_pieces[1:])
+    )
+    gate_pieces[1:], up_pieces[1:], down_pieces[1:], qkv_pieces[1:] = late
+    gate_pieces[0], up_pieces[0] = [from_replicas(part) for part in pending]
+    gate_pieces, up_pieces, down_pieces = [
+        [in_order(blocks) for blocks in pieces]
+        for pieces in (gate_pieces, up_pieces, down_pieces)
+    ]
+    qkv_pieces[1:] = [
+        jnp.concatenate(in_order(blocks), axis=0).astype(jnp.float32) for blocks in qkv_pieces[1:]
+    ]
     grad_gate_up = []
     for gates, ups in zip(gate_pieces, up_pieces):
         pairs = [
@@ -1082,16 +1105,17 @@
         grad_gate_up.append(join_blocks(pairs, hidden_width))
     grad_gate_up = jnp.stack(grad_gate_up)
     grad_down = jnp.stack([join_blocks(blocks, hidden_width) for blocks in down_pieces])
-    grad_both = jnp.stack(qkv_pieces)
-    grad_qkv = grad_both[:, :, :joined_width]
-    grad_out_proj = grad_both[:, :, joined_width:]
     bias = jnp.stack(bias_grads)
     slots = jnp.arange(cores, dtype=jnp.int32)[:, None, None] == core
     bias_slots = jnp.where(slots, bias[None], 0.0)
     gains_own = jnp.stack(gain_grads)
     small = jnp.concatenate([gains_own.reshape(-1), bias_slots.reshape(-1)])
-    small, _ = lax.optimization_barrier((small, both_sum))
+    small, both_sum = lax.optimization_barrier((small, both_sum))
+    qkv_pieces[0] = both_sum.astype(jnp.float32)
     small = sum_everywhere(small.reshape(-1, LANES), ("rep", "shard", "tp"), 7).reshape(-1)
+    grad_both = jnp.stack(qkv_pieces)
+    grad_qkv = grad_both[:, :, :joined_width]
+    grad_out_proj = grad_both[:, :, joined_width:]
     gains_total = small[: gains_own.size].reshape(gains_own.shape)
     bias_slots = small[gains_own.size :].reshape(bias_slots.shape)
     bias_total = lax.dynamic_index_in_dim(bias_slots, core, 0, keepdims=False)

time: 1710 us -> 1540 us (0.901)
  waiting for transfers between devices: 449 us -> 192 us
  Pallas kernels: 641 us -> 748 us
    reduce_scatter x8, waiting for transfers between devices: 289 us -> 109 us  [scattered(): return lax.psum_scatter(grad, axes, scatter_dimension=0, tiled=True)]
    pallas_call x24, Pallas kernels: 641 us -> 748 us  [call_kernel(): pl.pallas_call(kernel, out_shape=out_shape, in_specs=[pl.BlockSpec(memory...]
    ppermute x21, waiting for transfers between devices: 152 us -> 80.9 us  [from_replicas(): lax.ppermute(part, 'rep', peer_pairs(count, step))]
    optimization_barrier x5 -> x1, local copies, waits for them, and re-layouts: 26.1 us -> 0.3 us  [body(): mixed_grad, wide = lax.optimization_barrier((mixed_grad, pending[2]))]
    slice x2 -> x0, other arithmetic: 22.4 us -> none  [body(): gate_total = left_product(plane_rows, entry_grad[:, :block])]
    unnamed x283 -> x277, local copies, waits for them, and re-layouts: 41.9 us -> 40.1 us
  transfers between devices with their start and end apart: 33 -> 32, of which waited for: 19 -> 9; matrix products, arithmetic and copies ran while one was open for 18% -> 23% of each run, Pallas kernels for 33% -> 49%
where the time goes in v2:
time: 1540 us; the launch traced here: 1530 us
  Pallas kernels  748 us (49%)
  matrix products  283 us (18%)
  waiting for transfers between devices  192 us (12%)
  other arithmetic  145 us (9%)
  local copies, waits for them, and re-layouts  114 us (7%)
  starting transfers between devices  27.4 us (2%)
  between operations  17.4 us (1%)
    pallas_call x24, Pallas kernels, call_kernel(): pl.pallas_call(kernel, out_shape=out_shape, in_specs=[pl.BlockSpec(memory...  748 us
    reduce_scatter x8, waiting for transfers between devices, scattered(): return lax.psum_scatter(grad, axes, scatter_dimension=0, tiled=True)  109 us
    dot_general x10, matrix products, product(): return jnp.dot(left, right, preferred_element_type=jnp.float32)  86.7 us
    ppermute x21, waiting for transfers between devices, from_replicas(): lax.ppermute(part, 'rep', peer_pairs(count, step))  80.9 us
    dot_general x12, matrix products, right_product(): lax.dot_general(left, right, (((1,), (1,)), ((), ())), preferred_element_...  68.7 us
    dot_general x10, matrix products, left_product(): lax.dot_general(left, right, (((0,), (0,)), ((), ())), preferred_element_...  63.3 us
    unnamed x277, local copies, waits for them, and re-layouts  40.1 us
  transfers between devices with their start and end apart: 32, of which 9 were waited for; matrix products, arithmetic and copies ran while one was open for 23% of the time, Pallas kernels for 49%

profile of v2, /device:TPU:0, one launch (start us, length us, event | category | flops | bytes accessed | tf_op | source)
XLA Modules:
  0.0 1526.7 jit_solution(17251489689553221094)
XLA Ops:
  7.2 13.8 broadcast_select_fusion
  35.8 149.2 %shard_map.161 = bf16[4,4,96,3584]{3,2,1,0:T(8,128)(2,1)S(1)} custom-call(bf16[4,96,3584]{2,1,0:T(8,128)(2,1)S(1)} %pad_maximum_fusion.10.w_ref), custom_call_target="tpu_custom_call" | custom-call | bytes 150000000 | tf_op jit(solution)/shard_map/pallas_call | solution.py:147
  206.0 81.4 %shard_map.162 = bf16[4,768,128]{2,1,0:T(8,128)(2,1)S(1)} custom-call(bf16[768,128]{1,0:T(8,128)(2,1)S(1)} %bitcast.479), custom_call_target="tpu_custom_call" | custom-call | bytes 36000000 | tf_op jit(solution)/shard_map/pallas_call | solution.py:147
  306.3 25.3 %shard_map.164 = bf16[2,4,192,1536]{3,2,1,0:T(8,128)(2,1)S(1)} custom-call(bf16[192,1536]{1,0:T(8,128)(2,1)S(1)} %multiply_convert_fusion.9.x_ref), custom_call_target="tpu_custom_call" | custom-call | bytes 90000000 | tf_op jit(solution)/shard_map/pallas_call | solution.py:147
  334.2 25.1 %shard_map.172 = bf16[2,4,192,1536]{3,2,1,0:T(8,128)(2,1)S(1)} custom-call(bf16[192,1536]{1,0:T(8,128)(2,1)S(1)} %fusion.127.x_ref), custom_call_target="tpu_custom_call" | custom-call | bytes 90000000 | tf_op jit(solution)/shard_map/pallas_call | solution.py:147
  361.4 11.0 fusion.24
  372.4 11.2 multiply_convert_fusion.5
  393.1 25.0 %shard_map.165 = f32[192,1536]{1,0:T(8,128)S(1)} custom-call(bf16[1,4,192,1536]{3,2,1,0:T(8,128)(2,1)S(1)} %bitcast.470, f32[4,192,1536]{2,1,0:T(8,128)S(1)} %bitcast.462), custom_call_target="tpu_custom_call" | custom-call | bytes 84000000 | tf_op jit(solution)/shard_map/pallas_call | solution.py:147
  427.4 39.8 %shard_map.167 = bf16[4,768,128]{2,1,0:T(8,128)(2,1)S(1)} custom-call(bf16[768,128]{1,0:T(8,128)(2,1)S(1)} %bitcast.480), custom_call_target="tpu_custom_call" | custom-call | bytes 36000000 | tf_op jit(solution)/shard_map/pallas_call | solution.py:147
  484.5 24.7 %shard_map.169 = bf16[2,4,192,1536]{3,2,1,0:T(8,128)(2,1)S(1)} custom-call(bf16[192,1536]{1,0:T(8,128)(2,1)S(1)} %multiply_convert_fusion.7.x_ref), custom_call_target="tpu_custom_call" | custom-call | bytes 90000000 | tf_op jit(solution)/shard_map/pallas_call | solution.py:147
  511.5 10.8 fusion.20
  522.3 11.5 multiply_convert_fusion.4
  535.7 7.8 convolution_convert_fusion.5
  543.5 15.4 %multiply_convert_fusion.3 = (bf16[1536,1152]{0,1:T(8,128)(2,1)}, bf16[1536,1152]{0,1:T(8,128)(2,1)S(1)}) fusion(f32[1536,1152]{0,1:T(8,128)} %get-tuple-element.220, f32[1536,1152]{0,1:T(8,128)} %fusion.20, bf16[1536,1536]{1,0:T(8,128)(2,1)} %bitcast.447, bf16[1536,3456]{1,0:T(8,128)(2,1)} %all-gather.7.cloned.1.call-done), kind=kOutput, calls=%fused_computation.34 | convolution fusion | flops 5457051648 | bytes 29491200 | tf_op jit(solution)/shard_map/dot_general | solution.py:90
  560.6 7.7 convolution_convert_fusion.3
  568.4 10.4 convolution_convert_fusion.4
  597.6 24.5 %shard_map.170 = f32[192,1536]{1,0:T(8,128)S(1)} custom-call(bf16[1,4,192,1536]{3,2,1,0:T(8,128)(2,1)S(1)} %bitcast.469, f32[4,192,1536]{2,1,0:T(8,128)S(1)} %bitcast.461), custom_call_target="tpu_custom_call" | custom-call | bytes 84000000 | tf_op jit(solution)/shard_map/pallas_call | solution.py:147
  622.2 8.0 fusion.12
  630.2 8.0 fusion.44
  638.2 24.3 %shard_map.173 = f32[192,1536]{1,0:T(8,128)S(1)} custom-call(bf16[1,4,192,1536]{3,2,1,0:T(8,128)(2,1)S(1)} %bitcast.467, f32[4,192,1536]{2,1,0:T(8,128)S(1)} %bitcast.459), custom_call_target="tpu_custom_call" | custom-call | bytes 84000000 | tf_op jit(solution)/shard_map/pallas_call | solution.py:147
  671.7 12.9 fusion.3
  699.0 7.5 convolution_bitcast_fusion.2
  709.4 32.5 %shard_map.175 = f32[768,128]{1,0:T(8,128)S(1)} custom-call(bf16[3,768,128]{2,1,0:T(8,128)(2,1)S(1)} %bitcast.465, f32[768,128]{1,0:T(8,128)S(1)} %bitcast.471), custom_call_target="tpu_custom_call" | custom-call | bytes 42000000 | tf_op jit(solution)/shard_map/pallas_call | solution.py:147
  760.2 8.1 copy.158
  779.8 60.5 %reduce-scatter.15.cloned.1.call-done = bf16[384,1792]{1,0:T(8,128)(2,1)} async-done(((bf16[1536,1792]{1,0:T(8,128)(2,1)}), bf16[384,1792]{1,0:T(8,128)(2,1)}) %reduce-scatter.15.cloned.1.call-update) | async-done | bytes 1376272 | tf_op jit(solution)/shard_map/reduce_scatter | solution.py:806
  845.9 25.2 %shard_map.177 = bf16[2,4,192,1536]{3,2,1,0:T(8,128)(2,1)S(1)} custom-call(bf16[192,1536]{1,0:T(8,128)(2,1)S(1)} %get-tuple-element.110.x_ref), custom_call_target="tpu_custom_call" | custom-call | bytes 90000000 | tf_op jit(solution)/shard_map/pallas_call | solution.py:147
  873.4 7.7 convolution_convert_fusion.2
  881.1 27.9 %reduce-scatter.11.cloned.1.call-done = bf16[384,1152]{1,0:T(8,128)(2,1)} async-done(((bf16[1536,1152]{1,0:T(8,128)(2,1)}), bf16[384,1152]{1,0:T(8,128)(2,1)}) %reduce-scatter.11.cloned.1.call-update) | async-done | bytes 884752 | tf_op jit(solution)/shard_map/reduce_scatter | solution.py:806
  909.5 15.8 %multiply_convert_fusion.1 = (bf16[1536,1152]{0,1:T(8,128)(2,1)}, bf16[1536,1152]{0,1:T(8,128)(2,1)}) fusion(f32[1536,1152]{0,1:T(8,128)} %get-tuple-element.216, f32[1536,1152]{0,1:T(8,128)} %fusion.24, bf16[1536,1536]{1,0:T(8,128)(2,1)} %bitcast.458, bf16[1,1536,1152]{2,1,0:T(8,128)(2,1)} %all-gather.9.cloned.1.call-done), kind=kOutput, calls=%fused_computation.32 | convolution fusion | flops 5457051648 | bytes 29491200 | tf_op jit(solution)/shard_map/dot_general | solution.py:90
  931.8 9.8 convolution_convert_fusion
  941.6 10.5 convolution_convert_fusion.1
  957.1 21.0 %reduce-scatter.13.cloned.1.call-done = bf16[384,1152]{1,0:T(8,128)(2,1)} async-done(((bf16[1536,1152]{1,0:T(8,128)(2,1)}), bf16[384,1152]{1,0:T(8,128)(2,1)}) %reduce-scatter.13.cloned.1.call-update) | async-done | bytes 884752 | tf_op jit(solution)/shard_map/reduce_scatter | solution.py:806
  984.5 9.3 fusion.32
  993.8 9.1 fusion.38
  1002.9 54.9 %shard_map.178 = f32[192,1536]{1,0:T(8,128)S(1)} custom-call(bf16[1,4,192,1536]{3,2,1,0:T(8,128)(2,1)S(1)} %bitcast.468, f32[4,192,1536]{2,1,0:T(8,128)S(1)} %bitcast.460), custom_call_target="tpu_custom_call" | custom-call | bytes 84000000 | tf_op jit(solution)/shard_map/pallas_call | solution.py:147
  1068.4 12.5 fusion
  1093.5 7.6 convolution_bitcast_fusion
  1101.6 29.3 %shard_map.180 = f32[768,128]{1,0:T(8,128)S(1)} custom-call(bf16[3,768,128]{2,1,0:T(8,128)(2,1)S(1)} %bitcast.466, f32[768,128]{1,0:T(8,128)S(1)} %bitcast.472), custom_call_target="tpu_custom_call" | custom-call | bytes 42000000 | tf_op jit(solution)/shard_map/pallas_call | solution.py:147
  1156.9 16.0 %collective-permute-done.2 = bf16[384,1152]{1,0:T(8,128)(2,1)} collective-permute-done((bf16[384,1152]{1,0:T(8,128)(2,1)}, bf16[384,1152]{1,0:T(8,128)(2,1)}, u32[]{:S(2)}, u32[]{:S(2)}) %collective-permute-start.2) | collective-permute-done | bytes 884768 | tf_op jit(solution)/shard_map/ppermute | solution.py:776
  1174.4 17.4 %collective-permute-done.6 = bf16[384,1152]{1,0:T(8,128)(2,1)} collective-permute-done((bf16[384,1152]{1,0:T(8,128)(2,1)S(1)}, bf16[384,1152]{1,0:T(8,128)(2,1)}, u32[]{:S(2)}, u32[]{:S(2)}) %collective-permute-start.6) | collective-permute-done | bytes 884768 | tf_op jit(solution)/shard_map/ppermute | solution.py:776
  1192.5 8.3 copy.171
  1203.3 103.0 %shard_map.183 = bf16[4,96,1792]{2,1,0:T(8,128)(2,1)S(1)} custom-call(bf16[4,4,96,1792]{3,2,1,0:T(8,128)(2,1)S(1)} %bitcast.426), custom_call_target="tpu_custom_call" | custom-call | bytes 270000000 | tf_op jit(solution)/shard_map/pallas_call | solution.py:147
  1324.7 63.1 %shard_map.184 = f32[80,128]{1,0:T(8,128)S(1)} custom-call(f32[80,128]{1,0:T(8,128)S(1)} %bitcast.481), custom_call_target="tpu_custom_call" | custom-call | bytes 24000000 | tf_op jit(solution)/shard_map/pallas_call | solution.py:147
  1428.5 13.8 collective-permute-done.14
  1445.9 14.4 collective-permute-done.15
  1461.1 18.4 %collective-permute-done.17 = bf16[384,1152]{1,0:T(8,128)(2,1)S(1)} collective-permute-done((bf16[384,1152]{1,0:T(8,128)(2,1)S(1)}, bf16[384,1152]{1,0:T(8,128)(2,1)S(1)}, u32[]{:S(2)}, u32[]{:S(2)}) %collective-permute-start.17) | collective-permute-done | bytes 884768 | tf_op jit(solution)/shard_map/ppermute | solution.py:776
  1497.1 9.3 maximum_convert_fusion.1
  1506.4 13.5 maximum_convert_fusion
  (563 shorter events, 334.9 us)
Async XLA Ops:
  7.2 354.2 %all-gather.5.cloned.1.call-start = ((), (), s32[]{:S(2)}) async-start(), calls=%async_computation.8 | async-start | bytes 8847360 | tf_op jit(solution)/shard_map/all_gather | solution.py:802
  25.4 358.1 %all-gather.9.cloned.1.call-start = ((), (), s32[]{:S(2)}) async-start(), calls=%async_computation.18 | async-start | bytes 4423680 | tf_op jit(solution)/shard_map/all_gather | solution.py:802
  29.2 482.3 %all-gather.7.cloned.1.call-start = ((), (), s32[]{:S(2)}) async-start(), calls=%async_computation.9 | async-start | bytes 13271040 | tf_op jit(solution)/shard_map/all_gather | solution.py:802
  31.2 713.6 %reduce-scatter.9.cloned.1.call-start = ((), (), s32[]{:S(2)}) async-start(), calls=%async_computation.10 | async-start | bytes 4423680 | tf_op jit(solution)/shard_map/reduce_scatter | solution.py:806
  34.9 151.9 %copy-start.39 = (bf16[1,384,1536]{2,1,0:T(8,128)(2,1)}, bf16[1,384,1536]{2,1,0:T(8,128)(2,1)S(1)}, u32[]{:S(2)}) copy-start(bf16[1,384,1536]{2,1,0:T(8,128)(2,1)S(1)} %get-tuple-element.121) | copy-start | bytes 3538948
  35.3 151.6 %copy-start.108 = (f32[384]{0:T(512)}, f32[384]{0:T(512)S(1)}, u32[]{:S(2)}) copy-start(f32[384]{0:T(512)S(1)} %add_rsqrt_fusion) | copy-start | bytes 4612
  35.7 149.2 %copy-start.102 = (bf16[2,2,1536]{2,1,0:T(2,128)(2,1)S(1)}, bf16[2,2,1536]{2,1,0:T(2,128)(2,1)}, u32[]{:S(2)}) copy-start(bf16[2,2,1536]{2,1,0:T(2,128)(2,1)} %param.16) | copy-start | bytes 36868
  35.8 150.0 %copy-start.97 = (bf16[2,1024]{1,0:T(2,128)(2,1)S(1)}, bf16[2,1024]{1,0:T(2,128)(2,1)}, u32[]{:S(2)}) copy-start(bf16[2,1024]{1,0:T(2,128)(2,1)} %param.12) | copy-start | bytes 12292
  185.7 120.4 %copy-start.83 = (f32[1536]{0:T(1024)}, f32[1536]{0:T(1024)S(1)}, u32[]{:S(2)}) copy-start(f32[1536]{0:T(1024)S(1)} %get-tuple-element.102) | copy-start | bytes 18436
  185.7 233.2 %copy-start.85 = (f32[1536]{0:T(1024)}, f32[1536]{0:T(1024)S(1)}, u32[]{:S(2)}) copy-start(f32[1536]{0:T(1024)S(1)} %get-tuple-element.101) | copy-start | bytes 18436
  192.8 94.6 %copy-start.63 = (f32[1,1,384,1,64]{4,2,3,1,0:T(8,128)}, f32[1,1,384,1,64]{4,2,3,1,0:T(8,128)S(1)}, u32[]{:S(2)}) copy-start(f32[1,1,384,1,64]{4,2,3,1,0:T(8,128)S(1)} %get-tuple-element.204) | copy-start | bytes 294916
  204.2 83.3 %copy-start.91 = (s32[1536]{0:T(1024)S(1)}, s32[1536]{0:T(1024)}, u32[]{:S(2)}) copy-start(s32[1536]{0:T(1024)} %copy-done.90) | copy-start | bytes 18436
  204.2 83.3 %copy-start.92 = (s32[1536]{0:T(1024)S(1)}, s32[1536]{0:T(1024)}, u32[]{:S(2)}) copy-start(s32[1536]{0:T(1024)} %fusion.143) | copy-start | bytes 18436
  204.2 83.3 %copy-start.93 = (s32[384]{0:T(512)S(1)}, s32[384]{0:T(512)}, u32[]{:S(2)}) copy-start(s32[384]{0:T(512)} %get-tuple-element.202) | copy-start | bytes 4612
  204.2 83.3 %copy-start.95 = (s32[384]{0:T(512)S(1)}, s32[384]{0:T(512)}, u32[]{:S(2)}) copy-start(s32[384]{0:T(512)} %copy-done.94) | copy-start | bytes 4612
  204.2 83.3 %copy-start.103 = (pred[1536]{0:T(1024)(128)(4,1)S(1)}, pred[1536]{0:T(1024)(128)(4,1)}, u32[]{:S(2)}) copy-start(pred[1536]{0:T(1024)(128)(4,1)} %broadcast_compare_fusion) | copy-start | bytes 4612
  204.2 83.3 %copy-start.110 = (pred[384]{0:T(512)(128)(4,1)S(1)}, pred[384]{0:T(512)(128)(4,1)}, u32[]{:S(2)}) copy-start(pred[384]{0:T(512)(128)(4,1)} %broadcast_compare_fusion.1) | copy-start | bytes 1156
  204.2 85.0 %copy-start.59 = (f32[384,128]{0,1:T(8,128)S(1)}, f32[384,128]{0,1:T(8,128)}, u32[]{:S(2)}) copy-start(f32[384,128]{0,1:T(8,128)} %copy.135) | copy-start | bytes 589828
  204.2 85.0 %copy-start.61 = (f32[384,128]{0,1:T(8,128)S(1)}, f32[384,128]{0,1:T(8,128)}, u32[]{:S(2)}) copy-start(f32[384,128]{0,1:T(8,128)} %copy.136) | copy-start | bytes 589828
  305.6 112.5 %copy-start.14 = (f32[192,1536]{1,0:T(8,128)}, f32[192,1536]{1,0:T(8,128)S(1)}, u32[]{:S(2)}) copy-start(f32[192,1536]{1,0:T(8,128)S(1)} %get-tuple-element.119) | copy-start | bytes 3538948
  585.2 255.1 %reduce-scatter.15.cloned.1.call-start = ((), (), s32[]{:S(2)}) async-start(), calls=%async_computation.13 | async-start | bytes 6881280 | tf_op jit(solution)/shard_map/reduce_scatter | solution.py:806
  773.6 135.4 %reduce-scatter.11.cloned.1.call-start = ((), (), s32[]{:S(2)}) async-start(), calls=%async_computation.11 | async-start | bytes 4423680 | tf_op jit(solution)/shard_map/reduce_scatter | solution.py:806
  774.2 203.9 %reduce-scatter.13.cloned.1.call-start = ((), (), s32[]{:S(2)}) async-start(), calls=%async_computation.12 | async-start | bytes 4423680 | tf_op jit(solution)/shard_map/reduce_scatter | solution.py:806
  775.0 292.5 %reduce-scatter.17.cloned.1.call-start = ((), (), s32[]{:S(2)}) async-start(), calls=%async_computation.14 | async-start | bytes 1720320 | tf_op jit(solution)/shard_map/reduce_scatter | solution.py:806
  840.3 290.6 %reduce-scatter.19.cloned.1.call-start = ((), (), s32[]{:S(2)}) async-start(), calls=%async_computation.15 | async-start | bytes 4423680 | tf_op jit(solution)/shard_map/reduce_scatter | solution.py:806
  909.0 397.3 %reduce-scatter.21.cloned.1.call-start = ((), (), s32[]{:S(2)}) async-start(), calls=%async_computation.16 | async-start | bytes 4423680 | tf_op jit(solution)/shard_map/reduce_scatter | solution.py:806
  952.2 354.2 %reduce-scatter.23.cloned.1.call-start = ((), (), s32[]{:S(2)}) async-start(), calls=%async_computation.17 | async-start | bytes 4423680 | tf_op jit(solution)/shard_map/reduce_scatter | solution.py:806
  978.1 171.0 %collective-permute-start.3 = (bf16[384,1152]{1,0:T(8,128)(2,1)}, bf16[384,1152]{1,0:T(8,128)(2,1)}, u32[]{:S(2)}, u32[]{:S(2)}) collective-permute-start(bf16[384,1152]{1,0:T(8,128)(2,1)} %reduce-scatter.13.cloned.1.call-done), channel_id=1, source_target_pairs={{0,8},{8,0},{16,24},{24,16},{1,9},{9,1},{17,25},{25,17},{2,10},{10... | collective-permute-start | bytes 2654216 | tf_op jit(solution)/shard_map/ppermute | solution.py:776
  979.5 171.1 %collective-permute-start.4 = (bf16[384,1152]{1,0:T(8,128)(2,1)}, bf16[384,1152]{1,0:T(8,128)(2,1)}, u32[]{:S(2)}, u32[]{:S(2)}) collective-permute-start(bf16[384,1152]{1,0:T(8,128)(2,1)} %reduce-scatter.13.cloned.1.call-done), channel_id=1, source_target_pairs={{0,16},{8,24},{16,0},{24,8},{1,17},{9,25},{17,1},{25,9},{2,18},{10... | collective-permute-start | bytes 2654216 | tf_op jit(solution)/shard_map/ppermute | solution.py:776
  981.0 171.1 %collective-permute-start.5 = (bf16[384,1152]{1,0:T(8,128)(2,1)}, bf16[384,1152]{1,0:T(8,128)(2,1)}, u32[]{:S(2)}, u32[]{:S(2)}) collective-permute-start(bf16[384,1152]{1,0:T(8,128)(2,1)} %reduce-scatter.13.cloned.1.call-done), channel_id=1, source_target_pairs={{0,24},{8,16},{16,8},{24,0},{1,25},{9,17},{17,9},{25,1},{2,26},{10... | collective-permute-start | bytes 2654216 | tf_op jit(solution)/shard_map/ppermute | solution.py:776
  981.6 171.3 %collective-permute-start = (bf16[384,1152]{1,0:T(8,128)(2,1)}, bf16[384,1152]{1,0:T(8,128)(2,1)}, u32[]{:S(2)}, u32[]{:S(2)}) collective-permute-start(bf16[384,1152]{1,0:T(8,128)(2,1)} %reduce-scatter.11.cloned.1.call-done), channel_id=1, source_target_pairs={{0,8},{8,0},{16,24},{24,16},{1,9},{9,1},{17,25},{25,17},{2,10},{10... | collective-permute-start | bytes 2654216 | tf_op jit(solution)/shard_map/ppermute | solution.py:776
  983.0 173.3 %collective-permute-start.1 = (bf16[384,1152]{1,0:T(8,128)(2,1)}, bf16[384,1152]{1,0:T(8,128)(2,1)}, u32[]{:S(2)}, u32[]{:S(2)}) collective-permute-start(bf16[384,1152]{1,0:T(8,128)(2,1)} %reduce-scatter.11.cloned.1.call-done), channel_id=1, source_target_pairs={{0,16},{8,24},{16,0},{24,8},{1,17},{9,25},{17,1},{25,9},{2,18},{10... | collective-permute-start | bytes 2654216 | tf_op jit(solution)/shard_map/ppermute | solution.py:776
  1149.1 23.8 %collective-permute-start.2 = (bf16[384,1152]{1,0:T(8,128)(2,1)}, bf16[384,1152]{1,0:T(8,128)(2,1)}, u32[]{:S(2)}, u32[]{:S(2)}) collective-permute-start(bf16[384,1152]{1,0:T(8,128)(2,1)} %reduce-scatter.11.cloned.1.call-done), channel_id=1, source_target_pairs={{0,24},{8,16},{16,8},{24,0},{1,25},{9,17},{17,9},{25,1},{2,26},{10... | collective-permute-start | bytes 2654216 | tf_op jit(solution)/shard_map/ppermute | solution.py:776
  1150.6 41.2 %collective-permute-start.6 = (bf16[384,1152]{1,0:T(8,128)(2,1)S(1)}, bf16[384,1152]{1,0:T(8,128)(2,1)}, u32[]{:S(2)}, u32[]{:S(2)}) collective-permute-start(bf16[384,1152]{1,0:T(8,128)(2,1)S(1)} %copy-done.70), channel_id=1, source_target_pairs={{0,8},{8,0},{16,24},{24,16},{1,9},{9,1},{17,25},{25,17},{2,10},{10... | collective-permute-start | bytes 2654216 | tf_op jit(solution)/shard_map/ppermute | solution.py:776
  1152.2 159.4 %collective-permute-start.7 = (bf16[384,1152]{1,0:T(8,128)(2,1)S(1)}, bf16[384,1152]{1,0:T(8,128)(2,1)}, u32[]{:S(2)}, u32[]{:S(2)}) collective-permute-start(bf16[384,1152]{1,0:T(8,128)(2,1)S(1)} %copy-done.70), channel_id=1, source_target_pairs={{0,16},{8,24},{16,0},{24,8},{1,17},{9,25},{17,1},{25,9},{2,18},{10... | collective-permute-start | bytes 2654216 | tf_op jit(solution)/shard_map/ppermute | solution.py:776
  1152.8 162.4 %collective-permute-start.8 = (bf16[384,1152]{1,0:T(8,128)(2,1)S(1)}, bf16[384,1152]{1,0:T(8,128)(2,1)}, u32[]{:S(2)}, u32[]{:S(2)}) collective-permute-start(bf16[384,1152]{1,0:T(8,128)(2,1)S(1)} %copy-done.70), channel_id=1, source_target_pairs={{0,24},{8,16},{16,8},{24,0},{1,25},{9,17},{17,9},{25,1},{2,26},{10... | collective-permute-start | bytes 2654216 | tf_op jit(solution)/shard_map/ppermute | solution.py:776
  1156.3 159.2 %collective-permute-start.10 = (bf16[96,1792]{1,0:T(8,128)(2,1)}, bf16[96,1792]{1,0:T(8,128)(2,1)}, u32[]{:S(2)}, u32[]{:S(2)}) collective-permute-start(bf16[96,1792]{1,0:T(8,128)(2,1)} %reduce-scatter.17.cloned.1.call-done), channel_id=1, source_target_pairs={{0,16},{8,24},{16,0},{24,8},{1,17},{9,25},{17,1},{25,9},{2,18},{10... | collective-permute-start | bytes 1032200 | tf_op jit(solution)/shard_map/ppermute | solution.py:776
  1172.9 143.9 %collective-permute-start.11 = (bf16[96,1792]{1,0:T(8,128)(2,1)}, bf16[96,1792]{1,0:T(8,128)(2,1)}, u32[]{:S(2)}, u32[]{:S(2)}) collective-permute-start(bf16[96,1792]{1,0:T(8,128)(2,1)} %reduce-scatter.17.cloned.1.call-done), channel_id=1, source_target_pairs={{0,24},{8,16},{16,8},{24,0},{1,25},{9,17},{17,9},{25,1},{2,26},{10... | collective-permute-start | bytes 1032200 | tf_op jit(solution)/shard_map/ppermute | solution.py:776
  1191.8 126.9 %collective-permute-start.9 = (bf16[96,1792]{1,0:T(8,128)(2,1)}, bf16[96,1792]{1,0:T(8,128)(2,1)}, u32[]{:S(2)}, u32[]{:S(2)}) collective-permute-start(bf16[96,1792]{1,0:T(8,128)(2,1)} %reduce-scatter.17.cloned.1.call-done), channel_id=1, source_target_pairs={{0,8},{8,0},{16,24},{24,16},{1,9},{9,1},{17,25},{25,17},{2,10},{10... | collective-permute-start | bytes 1032200 | tf_op jit(solution)/shard_map/ppermute | solution.py:776
  1311.5 107.0 %collective-permute-start.18 = (bf16[384,1152]{1,0:T(8,128)(2,1)}, bf16[384,1152]{1,0:T(8,128)(2,1)}, u32[]{:S(2)}, u32[]{:S(2)}) collective-permute-start(bf16[384,1152]{1,0:T(8,128)(2,1)} %reduce-scatter.19.cloned.1.call-done), channel_id=1, source_target_pairs={{0,8},{8,0},{16,24},{24,16},{1,9},{9,1},{17,25},{25,17},{2,10},{10... | collective-permute-start | bytes 2654216 | tf_op jit(solution)/shard_map/ppermute | solution.py:776
  1315.3 104.5 %collective-permute-start.19 = (bf16[384,1152]{1,0:T(8,128)(2,1)}, bf16[384,1152]{1,0:T(8,128)(2,1)}, u32[]{:S(2)}, u32[]{:S(2)}) collective-permute-start(bf16[384,1152]{1,0:T(8,128)(2,1)} %reduce-scatter.19.cloned.1.call-done), channel_id=1, source_target_pairs={{0,16},{8,24},{16,0},{24,8},{1,17},{9,25},{17,1},{25,9},{2,18},{10... | collective-permute-start | bytes 2654216 | tf_op jit(solution)/shard_map/ppermute | solution.py:776
  1315.5 105.1 %collective-permute-start.20 = (bf16[384,1152]{1,0:T(8,128)(2,1)}, bf16[384,1152]{1,0:T(8,128)(2,1)}, u32[]{:S(2)}, u32[]{:S(2)}) collective-permute-start(bf16[384,1152]{1,0:T(8,128)(2,1)} %reduce-scatter.19.cloned.1.call-done), channel_id=1, source_target_pairs={{0,24},{8,16},{16,8},{24,0},{1,25},{9,17},{17,9},{25,1},{2,26},{10... | collective-permute-start | bytes 2654216 | tf_op jit(solution)/shard_map/ppermute | solution.py:776
  1316.8 110.5 %collective-permute-start.12 = (bf16[384,1152]{1,0:T(8,128)(2,1)}, bf16[384,1152]{1,0:T(8,128)(2,1)}, u32[]{:S(2)}, u32[]{:S(2)}) collective-permute-start(bf16[384,1152]{1,0:T(8,128)(2,1)} %reduce-scatter.21.cloned.1.call-done), channel_id=1, source_target_pairs={{0,8},{8,0},{16,24},{24,16},{1,9},{9,1},{17,25},{25,17},{2,10},{10... | collective-permute-start | bytes 2654216 | tf_op jit(solution)/shard_map/ppermute | solution.py:776
  1318.8 109.7 %collective-permute-start.13 = (bf16[384,1152]{1,0:T(8,128)(2,1)}, bf16[384,1152]{1,0:T(8,128)(2,1)}, u32[]{:S(2)}, u32[]{:S(2)}) collective-permute-start(bf16[384,1152]{1,0:T(8,128)(2,1)} %reduce-scatter.21.cloned.1.call-done), channel_id=1, source_target_pairs={{0,16},{8,24},{16,0},{24,8},{1,17},{9,25},{17,1},{25,9},{2,18},{10... | collective-permute-start | bytes 2654216 | tf_op jit(solution)/shard_map/ppermute | solution.py:776
  1418.6 23.7 %collective-permute-start.14 = (bf16[384,1152]{1,0:T(8,128)(2,1)}, bf16[384,1152]{1,0:T(8,128)(2,1)S(1)}, u32[]{:S(2)}, u32[]{:S(2)}) collective-permute-start(bf16[384,1152]{1,0:T(8,128)(2,1)} %reduce-scatter.21.cloned.1.call-done), channel_id=1, source_target_pairs={{0,24},{8,16},{16,8},{24,0},{1,25},{9,17},{17,9},{25,1},{2,26},{10... | collective-permute-start | bytes 2654216 | tf_op jit(solution)/shard_map/ppermute | solution.py:776
  1419.8 40.5 %collective-permute-start.15 = (bf16[384,1152]{1,0:T(8,128)(2,1)S(1)}, bf16[384,1152]{1,0:T(8,128)(2,1)S(1)}, u32[]{:S(2)}, u32[]{:S(2)}) collective-permute-start(bf16[384,1152]{1,0:T(8,128)(2,1)S(1)} %copy-done.73), channel_id=1, source_target_pairs={{0,8},{8,0},{16,24},{24,16},{1,9},{9,1},{17,25},{25,17},{2,10},{10... | collective-permute-start | bytes 2654216 | tf_op jit(solution)/shard_map/ppermute | solution.py:776
  1420.6 40.5 %collective-permute-start.16 = (bf16[384,1152]{1,0:T(8,128)(2,1)S(1)}, bf16[384,1152]{1,0:T(8,128)(2,1)S(1)}, u32[]{:S(2)}, u32[]{:S(2)}) collective-permute-start(bf16[384,1152]{1,0:T(8,128)(2,1)S(1)} %copy-done.73), channel_id=1, source_target_pairs={{0,16},{8,24},{16,0},{24,8},{1,17},{9,25},{17,1},{25,9},{2,18},{10... | collective-permute-start | bytes 2654216 | tf_op jit(solution)/shard_map/ppermute | solution.py:776
  1427.3 52.3 %collective-permute-start.17 = (bf16[384,1152]{1,0:T(8,128)(2,1)S(1)}, bf16[384,1152]{1,0:T(8,128)(2,1)S(1)}, u32[]{:S(2)}, u32[]{:S(2)}) collective-permute-start(bf16[384,1152]{1,0:T(8,128)(2,1)S(1)} %copy-done.73), channel_id=1, source_target_pairs={{0,24},{8,16},{16,8},{24,0},{1,25},{9,17},{17,9},{25,1},{2,26},{10... | collective-permute-start | bytes 2654216 | tf_op jit(solution)/shard_map/ppermute | solution.py:776
  (121 other events, 1517.6 us)
Sparse Core Ops, SparseCore 0:
  25.6 189.2 all-gather.4
  217.0 84.7 all-gather.8
  304.0 201.2 all-gather.6
  585.4 80.7 reduce-scatter.8
  773.8 66.5 reduce-scatter.14
  842.5 66.4 reduce-scatter.10
  911.3 66.6 reduce-scatter.12
  980.4 32.5 reduce-scatter.16
  1015.3 65.2 reduce-scatter.18
  1082.7 79.1 reduce-scatter.20
  1164.2 69.5 reduce-scatter.22

commit v3 on v2

--- a/solution.py
+++ b/solution.py
@@ -1005,7 +1005,7 @@
         plane_grad, down_total = lax.optimization_barrier((plane_grad, down_total))
         if pending is not None:
             plane_grad, part = lax.optimization_barrier((plane_grad, pending[0]))
-            gate_pieces[index + 1] = from_replicas(part)
+            up_pieces[index + 1] = from_replicas(part)
         hidden_grad = product(plane_grad, part_down)
         down_own = scattered(down_total)
         sigmoid = jax.nn.sigmoid(gate)
@@ -1017,9 +1017,6 @@
         entry_grad, gate_total, up_total = lax.optimization_barrier(
             (entry_grad, gate_total, up_total)
         )
-        if pending is not None:
-            entry_grad, part = lax.optimization_barrier((entry_grad, pending[1]))
-            up_pieces[index + 1] = from_replicas(part)
         own_parts = (scattered(gate_total), scattered(up_total))
         far_product = right_product(entry_grad[near_rows:], part_entry).astype(jnp.bfloat16)
         near_product = right_product(entry_grad[:near_rows], part_entry)
@@ -1029,9 +1026,11 @@
         out_grad = core_gather(middle_grad.astype(jnp.bfloat16), 3)
         mixed_grad = product(out_grad, full_out).astype(jnp.bfloat16)
         if pending is not None:
-            mixed_grad, wide = lax.optimization_barrier((mixed_grad, pending[2]))
+            mixed_grad, wide = lax.optimization_barrier((mixed_grad, pending[1]))
             qkv_pieces[index + 1] = from_replicas(wide)
-        pending = own_parts
+        if index:
+            mixed_grad, down_own = lax.optimization_barrier((mixed_grad, down_own))
+            down_pieces[index] = from_replicas(down_own)
         mixed_grad = mixed_grad.reshape(seqs, span, local_groups, group_index, HEAD_SIZE)
         attention_logits = masked_scores(query_rows, keys_all, seen, root)
         exact = jnp.exp(attention_logits - log_total)
@@ -1060,8 +1059,14 @@
         pair = pair.reshape(2, seqs, shards, span, local_groups, HEAD_SIZE)
         pair = jnp.moveaxis(pair, 2, 0).reshape(shards, -1, HEAD_SIZE)
         pair_own = ring_scatter(pair[1:].astype(jnp.bfloat16), pair[0], "shard", 6, 14)
-        pair_own, down_own = lax.optimization_barrier((pair_own, down_own))
-        down_pieces[index] = from_replicas(down_own)
+        if index:
+            pair_own, part = lax.optimization_barrier((pair_own, own_parts[0]))
+            gate_pieces[index] = from_replicas(part)
+            pending = own_parts[1:]
+        else:
+            pair_own, down_own = lax.optimization_barrier((pair_own, down_own))
+            down_pieces[index] = from_replicas(down_own)
+            pending = own_parts
         pair_own = pair_own.reshape(2, seqs, span, local_groups, HEAD_SIZE)
         key_own, value_own = pair_own[0], pair_own[1]
         unrotated_asks = rotate_back(query_grad, cos_query, sin_query)
@@ -1088,6 +1093,15 @@
         (both_sum, gate_pieces[1:], up_pieces[1:], down_pieces[1:], qkv_pieces[1:])
     )
     gate_pieces[1:], up_pieces[1:], down_pieces[1:], qkv_pieces[1:] = late
+    bias = jnp.stack(bias_grads)
+    slots = jnp.arange(cores, dtype=jnp.int32)[:, None, None] == core
+    bias_slots = jnp.where(slots, bias[None], 0.0)
+    gains_own = jnp.stack(gain_grads)
+    small = jnp.concatenate([gains_own.reshape(-1), bias_slots.reshape(-1)])
+    small, both_sum = lax.optimization_barrier((small, both_sum))
+    qkv_pieces[0] = both_sum.astype(jnp.float32)
+    small = sum_everywhere(small.reshape(-1, LANES), ("rep", "shard", "tp"), 7).reshape(-1)
+    small, *pending = lax.optimization_barrier((small, *pending))
     gate_pieces[0], up_pieces[0] = [from_replicas(part) for part in pending]
     gate_pieces, up_pieces, down_pieces = [
         [in_order(blocks) for blocks in pieces]
@@ -1105,14 +1119,6 @@
         grad_gate_up.append(join_blocks(pairs, hidden_width))
     grad_gate_up = jnp.stack(grad_gate_up)
     grad_down = jnp.stack([join_blocks(blocks, hidden_width) for blocks in down_pieces])
-    bias = jnp.stack(bias_grads)
-    slots = jnp.arange(cores, dtype=jnp.int32)[:, None, None] == core
-    bias_slots = jnp.where(slots, bias[None], 0.0)
-    gains_own = jnp.stack(gain_grads)
-    small = jnp.concatenate([gains_own.reshape(-1), bias_slots.reshape(-1)])
-    small, both_sum = lax.optimization_barrier((small, both_sum))
-    qkv_pieces[0] = both_sum.astype(jnp.float32)
-    small = sum_everywhere(small.reshape(-1, LANES), ("rep", "shard", "tp"), 7).reshape(-1)
     grad_both = jnp.stack(qkv_pieces)
     grad_qkv = grad_both[:, :, :joined_width]
     grad_out_proj = grad_both[:, :, joined_width:]

time: 1540 us -> 1490 us (0.968)
  waiting for transfers between devices: 192 us -> 167 us
    reduce_scatter x8, waiting for transfers between devices: 109 us -> 89 us  [scattered(): return lax.psum_scatter(grad, axes, scatter_dimension=0, tiled=True)]
    unnamed x277 -> x259, local copies, waits for them, and re-layouts: 40.1 us -> 39.2 us
  transfers between devices with their start and end apart: 32 -> 32, of which waited for: 9 -> 8; matrix products, arithmetic and copies ran while one was open for 23% -> 26% of each run, Pallas kernels for 49% -> 50%
where the time goes in v3:
time: 1490 us; the launch traced here: 1480 us
  Pallas kernels  737 us (49%)
  matrix products  284 us (19%)
  waiting for transfers between devices  167 us (11%)
  other arithmetic  144 us (10%)
  local copies, waits for them, and re-layouts  107 us (7%)
  starting transfers between devices  26.5 us (2%)
  between operations  17.4 us (1%)
    pallas_call x24, Pallas kernels, call_kernel(): pl.pallas_call(kernel, out_shape=out_shape, in_specs=[pl.BlockSpec(memory...  737 us
    reduce_scatter x8, waiting for transfers between devices, scattered(): return lax.psum_scatter(grad, axes, scatter_dimension=0, tiled=True)  89 us
    dot_general x10, matrix products, product(): return jnp.dot(left, right, preferred_element_type=jnp.float32)  87.1 us
    ppermute x21, waiting for transfers between devices, from_replicas(): lax.ppermute(part, 'rep', peer_pairs(count, step))  77.2 us
    dot_general x12, matrix products, right_product(): lax.dot_general(left, right, (((1,), (1,)), ((), ())), preferred_element_...  67 us
    dot_general x10, matrix products, left_product(): lax.dot_general(left, right, (((0,), (0,)), ((), ())), preferred_element_...  65.6 us
    unnamed x259, local copies, waits for them, and re-layouts  39.2 us
  transfers between devices with their start and end apart: 32, of which 8 were waited for; matrix products, arithmetic and copies ran while one was open for 26% of the time, Pallas kernels for 50%

profile of v3, /device:TPU:0, one launch (start us, length us, event | category | flops | bytes accessed | tf_op | source)
XLA Modules:
  0.0 1483.7 jit_solution(6772772949122079688)
XLA Ops:
  7.2 13.8 broadcast_select_fusion
  35.8 149.2 %shard_map.161 = bf16[4,4,96,3584]{3,2,1,0:T(8,128)(2,1)S(1)} custom-call(bf16[4,96,3584]{2,1,0:T(8,128)(2,1)S(1)} %pad_maximum_fusion.10.w_ref), custom_call_target="tpu_custom_call" | custom-call | bytes 150000000 | tf_op jit(solution)/shard_map/pallas_call | solution.py:147
  206.0 81.4 %shard_map.162 = bf16[4,768,128]{2,1,0:T(8,128)(2,1)S(1)} custom-call(bf16[768,128]{1,0:T(8,128)(2,1)S(1)} %bitcast.480), custom_call_target="tpu_custom_call" | custom-call | bytes 36000000 | tf_op jit(solution)/shard_map/pallas_call | solution.py:147
  306.5 25.3 %shard_map.164 = bf16[2,4,192,1536]{3,2,1,0:T(8,128)(2,1)S(1)} custom-call(bf16[192,1536]{1,0:T(8,128)(2,1)S(1)} %multiply_convert_fusion.9.x_ref), custom_call_target="tpu_custom_call" | custom-call | bytes 90000000 | tf_op jit(solution)/shard_map/pallas_call | solution.py:147
  334.4 25.0 %shard_map.172 = bf16[2,4,192,1536]{3,2,1,0:T(8,128)(2,1)S(1)} custom-call(bf16[192,1536]{1,0:T(8,128)(2,1)S(1)} %fusion.127.x_ref), custom_call_target="tpu_custom_call" | custom-call | bytes 90000000 | tf_op jit(solution)/shard_map/pallas_call | solution.py:147
  361.5 11.0 fusion.24
  372.5 11.3 multiply_convert_fusion.5
  393.4 25.0 %shard_map.165 = f32[192,1536]{1,0:T(8,128)S(1)} custom-call(bf16[1,4,192,1536]{3,2,1,0:T(8,128)(2,1)S(1)} %bitcast.471, f32[4,192,1536]{2,1,0:T(8,128)S(1)} %bitcast.463), custom_call_target="tpu_custom_call" | custom-call | bytes 84000000 | tf_op jit(solution)/shard_map/pallas_call | solution.py:147
  427.6 39.8 %shard_map.167 = bf16[4,768,128]{2,1,0:T(8,128)(2,1)S(1)} custom-call(bf16[768,128]{1,0:T(8,128)(2,1)S(1)} %bitcast.481), custom_call_target="tpu_custom_call" | custom-call | bytes 36000000 | tf_op jit(solution)/shard_map/pallas_call | solution.py:147
  484.8 24.7 %shard_map.169 = bf16[2,4,192,1536]{3,2,1,0:T(8,128)(2,1)S(1)} custom-call(bf16[192,1536]{1,0:T(8,128)(2,1)S(1)} %multiply_convert_fusion.7.x_ref), custom_call_target="tpu_custom_call" | custom-call | bytes 90000000 | tf_op jit(solution)/shard_map/pallas_call | solution.py:147
  511.7 10.8 fusion.20
  522.5 11.5 multiply_convert_fusion.4
  535.8 7.8 convolution_convert_fusion.5
  543.8 16.2 %multiply_convert_fusion.3 = (bf16[1536,1152]{0,1:T(8,128)(2,1)}, bf16[1536,1152]{0,1:T(8,128)(2,1)}) fusion(f32[1536,1152]{0,1:T(8,128)} %get-tuple-element.226, f32[1536,1152]{0,1:T(8,128)} %fusion.20, bf16[1536,1536]{1,0:T(8,128)(2,1)} %bitcast.448, bf16[1536,3456]{1,0:T(8,128)(2,1)} %all-gather.7.cloned.1.call-done), kind=kOutput, calls=%fused_computation.34 | convolution fusion | flops 5457051648 | bytes 29491200 | tf_op jit(solution)/shard_map/dot_general | solution.py:90
  566.4 9.8 convolution_convert_fusion.3
  576.1 10.7 convolution_convert_fusion.4
  598.5 24.5 %shard_map.170 = f32[192,1536]{1,0:T(8,128)S(1)} custom-call(bf16[1,4,192,1536]{3,2,1,0:T(8,128)(2,1)S(1)} %bitcast.470, f32[4,192,1536]{2,1,0:T(8,128)S(1)} %bitcast.462), custom_call_target="tpu_custom_call" | custom-call | bytes 84000000 | tf_op jit(solution)/shard_map/pallas_call | solution.py:147
  623.1 9.1 fusion.12
  632.2 9.0 fusion.44
  641.3 24.3 %shard_map.173 = f32[192,1536]{1,0:T(8,128)S(1)} custom-call(bf16[1,4,192,1536]{3,2,1,0:T(8,128)(2,1)S(1)} %bitcast.468, f32[4,192,1536]{2,1,0:T(8,128)S(1)} %bitcast.460), custom_call_target="tpu_custom_call" | custom-call | bytes 84000000 | tf_op jit(solution)/shard_map/pallas_call | solution.py:147
  675.8 12.9 fusion.3
  689.9 7.2 fusion.10
  702.6 7.6 convolution_bitcast_fusion.2
  712.8 31.6 %shard_map.175 = f32[768,128]{1,0:T(8,128)S(1)} custom-call(bf16[3,768,128]{2,1,0:T(8,128)(2,1)S(1)} %bitcast.466, f32[768,128]{1,0:T(8,128)S(1)} %bitcast.472), custom_call_target="tpu_custom_call" | custom-call | bytes 42000000 | tf_op jit(solution)/shard_map/pallas_call | solution.py:147
  760.3 8.0 copy.158
  779.3 60.8 %reduce-scatter.15.cloned.1.call-done = bf16[384,1792]{1,0:T(8,128)(2,1)} async-done(((bf16[1536,1792]{1,0:T(8,128)(2,1)}), bf16[384,1792]{1,0:T(8,128)(2,1)}) %reduce-scatter.15.cloned.1.call-update) | async-done | bytes 1376272 | tf_op jit(solution)/shard_map/reduce_scatter | solution.py:806
  845.8 25.2 %shard_map.177 = bf16[2,4,192,1536]{3,2,1,0:T(8,128)(2,1)S(1)} custom-call(bf16[192,1536]{1,0:T(8,128)(2,1)S(1)} %get-tuple-element.116.x_ref), custom_call_target="tpu_custom_call" | custom-call | bytes 90000000 | tf_op jit(solution)/shard_map/pallas_call | solution.py:147
  873.3 7.7 convolution_convert_fusion.2
  881.0 28.0 %reduce-scatter.13.cloned.1.call-done = bf16[384,1152]{1,0:T(8,128)(2,1)} async-done(((bf16[1536,1152]{1,0:T(8,128)(2,1)}), bf16[384,1152]{1,0:T(8,128)(2,1)}) %reduce-scatter.13.cloned.1.call-update) | async-done | bytes 884752 | tf_op jit(solution)/shard_map/reduce_scatter | solution.py:806
  909.1 15.9 %multiply_convert_fusion.1 = (bf16[1536,1152]{0,1:T(8,128)(2,1)}, bf16[1536,1152]{0,1:T(8,128)(2,1)}) fusion(f32[1536,1152]{0,1:T(8,128)} %get-tuple-element.222, f32[1536,1152]{0,1:T(8,128)} %fusion.24, bf16[1536,1536]{1,0:T(8,128)(2,1)} %bitcast.459, bf16[1,1536,1152]{2,1,0:T(8,128)(2,1)} %all-gather.9.cloned.1.call-done), kind=kOutput, calls=%fused_computation.32 | convolution fusion | flops 5457051648 | bytes 29491200 | tf_op jit(solution)/shard_map/dot_general | solution.py:90
  925.1 6.5 pad_maximum_fusion.1
  931.6 9.8 convolution_convert_fusion
  941.4 10.5 convolution_convert_fusion.1
  963.3 9.1 fusion.32
  978.5 58.9 %shard_map.178 = f32[192,1536]{1,0:T(8,128)S(1)} custom-call(bf16[1,4,192,1536]{3,2,1,0:T(8,128)(2,1)S(1)} %bitcast.469, f32[4,192,1536]{2,1,0:T(8,128)S(1)} %bitcast.461), custom_call_target="tpu_custom_call" | custom-call | bytes 84000000 | tf_op jit(solution)/shard_map/pallas_call | solution.py:147
  1047.9 12.5 fusion
  1060.4 7.1 fusion.11
  1073.2 7.6 convolution_bitcast_fusion
  1081.4 26.2 %shard_map.180 = f32[768,128]{1,0:T(8,128)S(1)} custom-call(bf16[3,768,128]{2,1,0:T(8,128)(2,1)S(1)} %bitcast.467, f32[768,128]{1,0:T(8,128)S(1)} %bitcast.473), custom_call_target="tpu_custom_call" | custom-call | bytes 42000000 | tf_op jit(solution)/shard_map/pallas_call | solution.py:147
  1132.9 16.4 %collective-permute-done.2 = bf16[384,1152]{1,0:T(8,128)(2,1)} collective-permute-done((bf16[384,1152]{1,0:T(8,128)(2,1)}, bf16[384,1152]{1,0:T(8,128)(2,1)}, u32[]{:S(2)}, u32[]{:S(2)}) %collective-permute-start.2) | collective-permute-done | bytes 884768 | tf_op jit(solution)/shard_map/ppermute | solution.py:776
  1150.7 17.4 %collective-permute-done.6 = bf16[384,1152]{1,0:T(8,128)(2,1)} collective-permute-done((bf16[384,1152]{1,0:T(8,128)(2,1)S(1)}, bf16[384,1152]{1,0:T(8,128)(2,1)}, u32[]{:S(2)}, u32[]{:S(2)}) %collective-permute-start.6) | collective-permute-done | bytes 884768 | tf_op jit(solution)/shard_map/ppermute | solution.py:776
  1168.8 8.3 copy.171
  1179.6 104.7 %shard_map.183 = bf16[4,96,1792]{2,1,0:T(8,128)(2,1)S(1)} custom-call(bf16[4,4,96,1792]{3,2,1,0:T(8,128)(2,1)S(1)} %bitcast.427), custom_call_target="tpu_custom_call" | custom-call | bytes 270000000 | tf_op jit(solution)/shard_map/pallas_call | solution.py:147
  1294.6 50.5 %shard_map.184 = f32[80,128]{1,0:T(8,128)S(1)} custom-call(f32[80,128]{1,0:T(8,128)S(1)} %bitcast.482), custom_call_target="tpu_custom_call" | custom-call | bytes 24000000 | tf_op jit(solution)/shard_map/pallas_call | solution.py:147
  1397.2 10.2 collective-permute-done.14
  1411.1 14.5 collective-permute-done.15
  1426.3 17.9 %collective-permute-done.17 = bf16[384,1152]{1,0:T(8,128)(2,1)S(1)} collective-permute-done((bf16[384,1152]{1,0:T(8,128)(2,1)S(1)}, bf16[384,1152]{1,0:T(8,128)(2,1)S(1)}, u32[]{:S(2)}, u32[]{:S(2)}) %collective-permute-start.17) | collective-permute-done | bytes 884768 | tf_op jit(solution)/shard_map/ppermute | solution.py:776
  1461.7 15.2 %maximum_convert_fusion = f32[2,384,2,4480]{3,2,1,0:T(2,128)} fusion(bf16[1,384,2,1024]{3,2,1,0:T(2,128)(2,1)} %slice_bitcast_fusion, bf16[1,384,2,1152]{3,2,1,0:T(2,128)(2,1)} %concatenate.336, bf16[1,384,2,1152]{3,2,1,0:T(2,128)(2,1)S(1)} %copy-done.26, bf16[1,384,2,1152]{3,2,1,0:T(2,128)(2,1)S(1)} %concatenate.332, ...), kind=kLoop, calls=%fused_computation.16 | loop fusion | flops 110100480 | bytes 41287680 | tf_op jit(solution)/shard_map/stack | solution.py:1120
  (544 shorter events, 317.2 us)
Async XLA Ops:
  7.2 354.4 %all-gather.5.cloned.1.call-start = ((), (), s32[]{:S(2)}) async-start(), calls=%async_computation.8 | async-start | bytes 8847360 | tf_op jit(solution)/shard_map/all_gather | solution.py:802
  25.4 358.4 %all-gather.9.cloned.1.call-start = ((), (), s32[]{:S(2)}) async-start(), calls=%async_computation.18 | async-start | bytes 4423680 | tf_op jit(solution)/shard_map/all_gather | solution.py:802
  29.2 482.5 %all-gather.7.cloned.1.call-start = ((), (), s32[]{:S(2)}) async-start(), calls=%async_computation.9 | async-start | bytes 13271040 | tf_op jit(solution)/shard_map/all_gather | solution.py:802
  31.2 644.3 %reduce-scatter.9.cloned.1.call-start = ((), (), s32[]{:S(2)}) async-start(), calls=%async_computation.10 | async-start | bytes 4423680 | tf_op jit(solution)/shard_map/reduce_scatter | solution.py:806
  34.9 151.9 %copy-start.33 = (bf16[1,384,1536]{2,1,0:T(8,128)(2,1)}, bf16[1,384,1536]{2,1,0:T(8,128)(2,1)S(1)}, u32[]{:S(2)}) copy-start(bf16[1,384,1536]{2,1,0:T(8,128)(2,1)S(1)} %get-tuple-element.127) | copy-start | bytes 3538948
  35.3 151.6 %copy-start.97 = (f32[384]{0:T(512)}, f32[384]{0:T(512)S(1)}, u32[]{:S(2)}) copy-start(f32[384]{0:T(512)S(1)} %add_rsqrt_fusion) | copy-start | bytes 4612
  35.7 149.2 %copy-start.91 = (bf16[2,2,1536]{2,1,0:T(2,128)(2,1)S(1)}, bf16[2,2,1536]{2,1,0:T(2,128)(2,1)}, u32[]{:S(2)}) copy-start(bf16[2,2,1536]{2,1,0:T(2,128)(2,1)} %param.16) | copy-start | bytes 36868
  35.8 150.0 %copy-start.86 = (bf16[2,1024]{1,0:T(2,128)(2,1)S(1)}, bf16[2,1024]{1,0:T(2,128)(2,1)}, u32[]{:S(2)}) copy-start(bf16[2,1024]{1,0:T(2,128)(2,1)} %param.12) | copy-start | bytes 12292
  185.7 120.6 %copy-start.72 = (f32[1536]{0:T(1024)}, f32[1536]{0:T(1024)S(1)}, u32[]{:S(2)}) copy-start(f32[1536]{0:T(1024)S(1)} %get-tuple-element.108) | copy-start | bytes 18436
  185.7 233.4 %copy-start.74 = (f32[1536]{0:T(1024)}, f32[1536]{0:T(1024)S(1)}, u32[]{:S(2)}) copy-start(f32[1536]{0:T(1024)S(1)} %get-tuple-element.107) | copy-start | bytes 18436
  192.8 94.7 %copy-start.53 = (f32[1,1,384,1,64]{4,2,3,1,0:T(8,128)}, f32[1,1,384,1,64]{4,2,3,1,0:T(8,128)S(1)}, u32[]{:S(2)}) copy-start(f32[1,1,384,1,64]{4,2,3,1,0:T(8,128)S(1)} %get-tuple-element.210) | copy-start | bytes 294916
  204.2 83.3 %copy-start.80 = (s32[1536]{0:T(1024)S(1)}, s32[1536]{0:T(1024)}, u32[]{:S(2)}) copy-start(s32[1536]{0:T(1024)} %copy-done.79) | copy-start | bytes 18436
  204.2 83.3 %copy-start.81 = (s32[1536]{0:T(1024)S(1)}, s32[1536]{0:T(1024)}, u32[]{:S(2)}) copy-start(s32[1536]{0:T(1024)} %fusion.143) | copy-start | bytes 18436
  204.2 83.3 %copy-start.82 = (s32[384]{0:T(512)S(1)}, s32[384]{0:T(512)}, u32[]{:S(2)}) copy-start(s32[384]{0:T(512)} %get-tuple-element.208) | copy-start | bytes 4612
  204.2 83.3 %copy-start.84 = (s32[384]{0:T(512)S(1)}, s32[384]{0:T(512)}, u32[]{:S(2)}) copy-start(s32[384]{0:T(512)} %copy-done.83) | copy-start | bytes 4612
  204.2 83.3 %copy-start.92 = (pred[1536]{0:T(1024)(128)(4,1)S(1)}, pred[1536]{0:T(1024)(128)(4,1)}, u32[]{:S(2)}) copy-start(pred[1536]{0:T(1024)(128)(4,1)} %broadcast_compare_fusion) | copy-start | bytes 4612
  204.3 83.3 %copy-start.99 = (pred[384]{0:T(512)(128)(4,1)S(1)}, pred[384]{0:T(512)(128)(4,1)}, u32[]{:S(2)}) copy-start(pred[384]{0:T(512)(128)(4,1)} %broadcast_compare_fusion.1) | copy-start | bytes 1156
  204.3 85.0 %copy-start.49 = (f32[384,128]{0,1:T(8,128)S(1)}, f32[384,128]{0,1:T(8,128)}, u32[]{:S(2)}) copy-start(f32[384,128]{0,1:T(8,128)} %copy.135) | copy-start | bytes 589828
  204.3 85.0 %copy-start.51 = (f32[384,128]{0,1:T(8,128)S(1)}, f32[384,128]{0,1:T(8,128)}, u32[]{:S(2)}) copy-start(f32[384,128]{0,1:T(8,128)} %copy.136) | copy-start | bytes 589828
  305.6 112.7 %copy-start.13 = (f32[192,1536]{1,0:T(8,128)}, f32[192,1536]{1,0:T(8,128)S(1)}, u32[]{:S(2)}) copy-start(f32[192,1536]{1,0:T(8,128)S(1)} %get-tuple-element.125) | copy-start | bytes 3538948
  543.7 200.7 %reduce-scatter.11.cloned.1.call-start = ((), (), s32[]{:S(2)}) async-start(), calls=%async_computation.11 | async-start | bytes 4423680 | tf_op jit(solution)/shard_map/reduce_scatter | solution.py:806
  623.1 217.1 %reduce-scatter.15.cloned.1.call-start = ((), (), s32[]{:S(2)}) async-start(), calls=%async_computation.13 | async-start | bytes 6881280 | tf_op jit(solution)/shard_map/reduce_scatter | solution.py:806
  773.7 135.3 %reduce-scatter.13.cloned.1.call-start = ((), (), s32[]{:S(2)}) async-start(), calls=%async_computation.12 | async-start | bytes 4423680 | tf_op jit(solution)/shard_map/reduce_scatter | solution.py:806
  774.5 272.5 %reduce-scatter.17.cloned.1.call-start = ((), (), s32[]{:S(2)}) async-start(), calls=%async_computation.14 | async-start | bytes 1720320 | tf_op jit(solution)/shard_map/reduce_scatter | solution.py:806
  840.2 267.4 %reduce-scatter.19.cloned.1.call-start = ((), (), s32[]{:S(2)}) async-start(), calls=%async_computation.15 | async-start | bytes 4423680 | tf_op jit(solution)/shard_map/reduce_scatter | solution.py:806
  909.1 375.3 %reduce-scatter.21.cloned.1.call-start = ((), (), s32[]{:S(2)}) async-start(), calls=%async_computation.16 | async-start | bytes 4423680 | tf_op jit(solution)/shard_map/reduce_scatter | solution.py:806
  952.0 332.4 %reduce-scatter.23.cloned.1.call-start = ((), (), s32[]{:S(2)}) async-start(), calls=%async_computation.17 | async-start | bytes 4423680 | tf_op jit(solution)/shard_map/reduce_scatter | solution.py:806
  956.9 168.5 %collective-permute-start.3 = (bf16[384,1152]{1,0:T(8,128)(2,1)}, bf16[384,1152]{1,0:T(8,128)(2,1)}, u32[]{:S(2)}, u32[]{:S(2)}) collective-permute-start(bf16[384,1152]{1,0:T(8,128)(2,1)} %reduce-scatter.13.cloned.1.call-done), channel_id=1, source_target_pairs={{0,8},{8,0},{16,24},{24,16},{1,9},{9,1},{17,25},{25,17},{2,10},{10... | collective-permute-start | bytes 2654216 | tf_op jit(solution)/shard_map/ppermute | solution.py:776
  958.4 168.6 %collective-permute-start.4 = (bf16[384,1152]{1,0:T(8,128)(2,1)}, bf16[384,1152]{1,0:T(8,128)(2,1)}, u32[]{:S(2)}, u32[]{:S(2)}) collective-permute-start(bf16[384,1152]{1,0:T(8,128)(2,1)} %reduce-scatter.13.cloned.1.call-done), channel_id=1, source_target_pairs={{0,16},{8,24},{16,0},{24,8},{1,17},{9,25},{17,1},{25,9},{2,18},{10... | collective-permute-start | bytes 2654216 | tf_op jit(solution)/shard_map/ppermute | solution.py:776
  959.8 168.7 %collective-permute-start.5 = (bf16[384,1152]{1,0:T(8,128)(2,1)}, bf16[384,1152]{1,0:T(8,128)(2,1)}, u32[]{:S(2)}, u32[]{:S(2)}) collective-permute-start(bf16[384,1152]{1,0:T(8,128)(2,1)} %reduce-scatter.13.cloned.1.call-done), channel_id=1, source_target_pairs={{0,24},{8,16},{16,8},{24,0},{1,25},{9,17},{17,9},{25,1},{2,26},{10... | collective-permute-start | bytes 2654216 | tf_op jit(solution)/shard_map/ppermute | solution.py:776
  960.4 168.8 %collective-permute-start = (bf16[384,1152]{1,0:T(8,128)(2,1)}, bf16[384,1152]{1,0:T(8,128)(2,1)}, u32[]{:S(2)}, u32[]{:S(2)}) collective-permute-start(bf16[384,1152]{1,0:T(8,128)(2,1)} %reduce-scatter.11.cloned.1.call-done), channel_id=1, source_target_pairs={{0,8},{8,0},{16,24},{24,16},{1,9},{9,1},{17,25},{25,17},{2,10},{10... | collective-permute-start | bytes 2654216 | tf_op jit(solution)/shard_map/ppermute | solution.py:776
  961.8 170.8 %collective-permute-start.1 = (bf16[384,1152]{1,0:T(8,128)(2,1)}, bf16[384,1152]{1,0:T(8,128)(2,1)}, u32[]{:S(2)}, u32[]{:S(2)}) collective-permute-start(bf16[384,1152]{1,0:T(8,128)(2,1)} %reduce-scatter.11.cloned.1.call-done), channel_id=1, source_target_pairs={{0,16},{8,24},{16,0},{24,8},{1,17},{9,25},{17,1},{25,9},{2,18},{10... | collective-permute-start | bytes 2654216 | tf_op jit(solution)/shard_map/ppermute | solution.py:776
  1125.4 23.8 %collective-permute-start.2 = (bf16[384,1152]{1,0:T(8,128)(2,1)}, bf16[384,1152]{1,0:T(8,128)(2,1)}, u32[]{:S(2)}, u32[]{:S(2)}) collective-permute-start(bf16[384,1152]{1,0:T(8,128)(2,1)} %reduce-scatter.11.cloned.1.call-done), channel_id=1, source_target_pairs={{0,24},{8,16},{16,8},{24,0},{1,25},{9,17},{17,9},{25,1},{2,26},{10... | collective-permute-start | bytes 2654216 | tf_op jit(solution)/shard_map/ppermute | solution.py:776
  1126.9 41.2 %collective-permute-start.6 = (bf16[384,1152]{1,0:T(8,128)(2,1)S(1)}, bf16[384,1152]{1,0:T(8,128)(2,1)}, u32[]{:S(2)}, u32[]{:S(2)}) collective-permute-start(bf16[384,1152]{1,0:T(8,128)(2,1)S(1)} %copy-done.60), channel_id=1, source_target_pairs={{0,8},{8,0},{16,24},{24,16},{1,9},{9,1},{17,25},{25,17},{2,10},{10... | collective-permute-start | bytes 2654216 | tf_op jit(solution)/shard_map/ppermute | solution.py:776
  1128.5 161.1 %collective-permute-start.7 = (bf16[384,1152]{1,0:T(8,128)(2,1)S(1)}, bf16[384,1152]{1,0:T(8,128)(2,1)}, u32[]{:S(2)}, u32[]{:S(2)}) collective-permute-start(bf16[384,1152]{1,0:T(8,128)(2,1)S(1)} %copy-done.60), channel_id=1, source_target_pairs={{0,16},{8,24},{16,0},{24,8},{1,17},{9,25},{17,1},{25,9},{2,18},{10... | collective-permute-start | bytes 2654216 | tf_op jit(solution)/shard_map/ppermute | solution.py:776
  1129.2 163.9 %collective-permute-start.8 = (bf16[384,1152]{1,0:T(8,128)(2,1)S(1)}, bf16[384,1152]{1,0:T(8,128)(2,1)}, u32[]{:S(2)}, u32[]{:S(2)}) collective-permute-start(bf16[384,1152]{1,0:T(8,128)(2,1)S(1)} %copy-done.60), channel_id=1, source_target_pairs={{0,24},{8,16},{16,8},{24,0},{1,25},{9,17},{17,9},{25,1},{2,26},{10... | collective-permute-start | bytes 2654216 | tf_op jit(solution)/shard_map/ppermute | solution.py:776
  1132.7 160.9 %collective-permute-start.10 = (bf16[96,1792]{1,0:T(8,128)(2,1)}, bf16[96,1792]{1,0:T(8,128)(2,1)}, u32[]{:S(2)}, u32[]{:S(2)}) collective-permute-start(bf16[96,1792]{1,0:T(8,128)(2,1)} %reduce-scatter.17.cloned.1.call-done), channel_id=1, source_target_pairs={{0,16},{8,24},{16,0},{24,8},{1,17},{9,25},{17,1},{25,9},{2,18},{10... | collective-permute-start | bytes 1032200 | tf_op jit(solution)/shard_map/ppermute | solution.py:776
  1149.3 145.4 %collective-permute-start.11 = (bf16[96,1792]{1,0:T(8,128)(2,1)}, bf16[96,1792]{1,0:T(8,128)(2,1)}, u32[]{:S(2)}, u32[]{:S(2)}) collective-permute-start(bf16[96,1792]{1,0:T(8,128)(2,1)} %reduce-scatter.17.cloned.1.call-done), channel_id=1, source_target_pairs={{0,24},{8,16},{16,8},{24,0},{1,25},{9,17},{17,9},{25,1},{2,26},{10... | collective-permute-start | bytes 1032200 | tf_op jit(solution)/shard_map/ppermute | solution.py:776
  1168.2 126.5 %collective-permute-start.9 = (bf16[96,1792]{1,0:T(8,128)(2,1)}, bf16[96,1792]{1,0:T(8,128)(2,1)}, u32[]{:S(2)}, u32[]{:S(2)}) collective-permute-start(bf16[96,1792]{1,0:T(8,128)(2,1)} %reduce-scatter.17.cloned.1.call-done), channel_id=1, source_target_pairs={{0,8},{8,0},{16,24},{24,16},{1,9},{9,1},{17,25},{25,17},{2,10},{10... | collective-permute-start | bytes 1032200 | tf_op jit(solution)/shard_map/ppermute | solution.py:776
  1289.6 94.2 %collective-permute-start.18 = (bf16[384,1152]{1,0:T(8,128)(2,1)}, bf16[384,1152]{1,0:T(8,128)(2,1)}, u32[]{:S(2)}, u32[]{:S(2)}) collective-permute-start(bf16[384,1152]{1,0:T(8,128)(2,1)} %reduce-scatter.19.cloned.1.call-done), channel_id=1, source_target_pairs={{0,8},{8,0},{16,24},{24,16},{1,9},{9,1},{17,25},{25,17},{2,10},{10... | collective-permute-start | bytes 2654216 | tf_op jit(solution)/shard_map/ppermute | solution.py:776
  1293.1 92.4 %collective-permute-start.19 = (bf16[384,1152]{1,0:T(8,128)(2,1)}, bf16[384,1152]{1,0:T(8,128)(2,1)}, u32[]{:S(2)}, u32[]{:S(2)}) collective-permute-start(bf16[384,1152]{1,0:T(8,128)(2,1)} %reduce-scatter.19.cloned.1.call-done), channel_id=1, source_target_pairs={{0,16},{8,24},{16,0},{24,8},{1,17},{9,25},{17,1},{25,9},{2,18},{10... | collective-permute-start | bytes 2654216 | tf_op jit(solution)/shard_map/ppermute | solution.py:776
  1293.6 92.3 %collective-permute-start.20 = (bf16[384,1152]{1,0:T(8,128)(2,1)}, bf16[384,1152]{1,0:T(8,128)(2,1)}, u32[]{:S(2)}, u32[]{:S(2)}) collective-permute-start(bf16[384,1152]{1,0:T(8,128)(2,1)} %reduce-scatter.19.cloned.1.call-done), channel_id=1, source_target_pairs={{0,24},{8,16},{16,8},{24,0},{1,25},{9,17},{17,9},{25,1},{2,26},{10... | collective-permute-start | bytes 2654216 | tf_op jit(solution)/shard_map/ppermute | solution.py:776
  1345.2 50.3 %collective-permute-start.12 = (bf16[384,1152]{1,0:T(8,128)(2,1)}, bf16[384,1152]{1,0:T(8,128)(2,1)}, u32[]{:S(2)}, u32[]{:S(2)}) collective-permute-start(bf16[384,1152]{1,0:T(8,128)(2,1)} %reduce-scatter.21.cloned.1.call-done), channel_id=1, source_target_pairs={{0,8},{8,0},{16,24},{24,16},{1,9},{9,1},{17,25},{25,17},{2,10},{10... | collective-permute-start | bytes 2654216 | tf_op jit(solution)/shard_map/ppermute | solution.py:776
  1345.7 51.6 %collective-permute-start.13 = (bf16[384,1152]{1,0:T(8,128)(2,1)}, bf16[384,1152]{1,0:T(8,128)(2,1)}, u32[]{:S(2)}, u32[]{:S(2)}) collective-permute-start(bf16[384,1152]{1,0:T(8,128)(2,1)} %reduce-scatter.21.cloned.1.call-done), channel_id=1, source_target_pairs={{0,16},{8,24},{16,0},{24,8},{1,17},{9,25},{17,1},{25,9},{2,18},{10... | collective-permute-start | bytes 2654216 | tf_op jit(solution)/shard_map/ppermute | solution.py:776
  1383.8 23.7 %collective-permute-start.14 = (bf16[384,1152]{1,0:T(8,128)(2,1)}, bf16[384,1152]{1,0:T(8,128)(2,1)S(1)}, u32[]{:S(2)}, u32[]{:S(2)}) collective-permute-start(bf16[384,1152]{1,0:T(8,128)(2,1)} %reduce-scatter.21.cloned.1.call-done), channel_id=1, source_target_pairs={{0,24},{8,16},{16,8},{24,0},{1,25},{9,17},{17,9},{25,1},{2,26},{10... | collective-permute-start | bytes 2654216 | tf_op jit(solution)/shard_map/ppermute | solution.py:776
  1385.5 40.1 %collective-permute-start.15 = (bf16[384,1152]{1,0:T(8,128)(2,1)S(1)}, bf16[384,1152]{1,0:T(8,128)(2,1)S(1)}, u32[]{:S(2)}, u32[]{:S(2)}) collective-permute-start(bf16[384,1152]{1,0:T(8,128)(2,1)S(1)} %copy-done.62), channel_id=1, source_target_pairs={{0,8},{8,0},{16,24},{24,16},{1,9},{9,1},{17,25},{25,17},{2,10},{10... | collective-permute-start | bytes 2654216 | tf_op jit(solution)/shard_map/ppermute | solution.py:776
  1385.9 40.4 %collective-permute-start.16 = (bf16[384,1152]{1,0:T(8,128)(2,1)S(1)}, bf16[384,1152]{1,0:T(8,128)(2,1)S(1)}, u32[]{:S(2)}, u32[]{:S(2)}) collective-permute-start(bf16[384,1152]{1,0:T(8,128)(2,1)S(1)} %copy-done.62), channel_id=1, source_target_pairs={{0,16},{8,24},{16,0},{24,8},{1,17},{9,25},{17,1},{25,9},{2,18},{10... | collective-permute-start | bytes 2654216 | tf_op jit(solution)/shard_map/ppermute | solution.py:776
  1395.5 48.7 %collective-permute-start.17 = (bf16[384,1152]{1,0:T(8,128)(2,1)S(1)}, bf16[384,1152]{1,0:T(8,128)(2,1)S(1)}, u32[]{:S(2)}, u32[]{:S(2)}) collective-permute-start(bf16[384,1152]{1,0:T(8,128)(2,1)S(1)} %copy-done.62), channel_id=1, source_target_pairs={{0,24},{8,16},{16,8},{24,0},{1,25},{9,17},{17,9},{25,1},{2,26},{10... | collective-permute-start | bytes 2654216 | tf_op jit(solution)/shard_map/ppermute | solution.py:776
  (110 other events, 1532.0 us)
Sparse Core Ops, SparseCore 0:
  25.6 189.2 all-gather.4
  217.0 84.7 all-gather.8
  304.0 201.2 all-gather.6
  543.8 80.8 reduce-scatter.8
  626.8 77.0 reduce-scatter.10
  773.8 66.3 reduce-scatter.14
  842.5 66.4 reduce-scatter.12
  911.4 32.5 reduce-scatter.16
  946.3 65.2 reduce-scatter.18
  1013.7 66.6 reduce-scatter.20
  1082.8 73.2 reduce-scatter.22
